TPU v7x, 32 devices: a whole 2x2x4 slice. The times are simulated.
32 devices in a mesh: grp: 2 (over x), row: 8 (over z, y), col: 2 (over core).
Axes of the slice: x: 2, y: 2, z: 4, core: 2. Of those that a mesh axis runs over, the one named last changes fastest.
Arguments:
- density: bfloat16 [1024, 32, 128], P(('grp', 'row', 'col')), parts along dimension 0, may hold values from -6 to 6
- leaf_target: int32 [1024], P(('grp', 'row', 'col')), parts along dimension 0, may hold values from 0 to 511, as said below
- geometry: float32 [6, 131072], P(None, ('grp', 'row', 'col')), parts along dimension 1, may hold values from -6 to 6
- near_list: int32 [1024, 16], P(('grp', 'row', 'col')), parts along dimension 0, may hold values from -1 to 511, as said below
- far_list: int32 [1024, 16], P(('grp', 'row', 'col')), parts along dimension 0, may hold values from -1 to 511, as said below
- node_list: int32 [128, 32], P(('grp', 'row', 'col')), parts along dimension 0, may hold values from -1 to 63, as said below
- basis_in: bfloat16 [1024, 64, 128], P(('grp', 'row', 'col')), parts along dimension 0, may hold values from -0.5 to 0.5
- basis_out: bfloat16 [1024, 64, 128], P(('grp', 'row', 'col')), parts along dimension 0, may hold values from -0.75 to 0.75
- transfer: bfloat16 [128, 64, 512], P(('grp', 'row', 'col')), parts along dimension 0, may hold values from -0.25 to 0.25
- node_points: float32 [3, 8192], P(None, 'grp'), parts along dimension 1, may hold values from -6 to 6
Outputs:
- potential: bfloat16 [1024, 32, 128], P(('grp', 'row', 'col')), parts along dimension 0
There are 2 independent parts, one for each index of `grp`. A program takes and returns all parts, laid end to end along the dimension named above; each array names one. Nothing has to cross between parts.
Inputs may be any that keep to these rules, and one draw needn't show every extreme that they name: `leaf_target`: A permutation of the tree positions; of the 32 slab leaves of one device, exactly 2 go to the block of 32 tree positions of each device. `near_list`: row t holds t in slot 0; every other slot holds either -1 or a leaf other than t within 16 of t, the leaves of a row distinct; a -1 may stand in any slot after slot 0, also between leaves. `far_list`: every slot of row t holds either -1 or a leaf within 16 of t that is neither t nor in row t of near_list, the leaves of a row distinct; a -1 may stand in any slot, also between leaves. `node_list`: row p holds distinct nodes that differ from p by more than 2, then -1 in the unused slots.
All inputs are finite; a program needn't handle non-finite values.
Results may differ from a plain program's by a relative error of at most 0.0053.
Values may be sent and summed in bfloat16 or wider, within the bound.
A program may use at most 64 MiB of HBM per device.

v0:
```python
import math

import jax
import jax.numpy as jnp
from jax import lax
from jax.sharding import PartitionSpec as P

REACH = 16


smoothing = 0.1
inv_four_pi = 0.25 / math.pi


def extended(cells, sides, width):
    for axis, dim in sides:
        count = lax.axis_size(axis)
        ends = count - 1
        head = lax.slice_in_dim(cells, 0, width, axis=dim)
        tail = lax.slice_in_dim(cells, cells.shape[dim] - width, cells.shape[dim], axis=dim)
        cells = jnp.concatenate(
            [
                lax.ppermute(tail, axis, [(i, (i + 1) % count) for i in range(ends)]),
                cells,
                lax.ppermute(head, axis, [((i + 1) % count, i) for i in range(ends)]),
            ],
            axis=dim,
        )
    return cells


def coupling(targets, sources):
    spread = targets - sources
    return inv_four_pi / jnp.sqrt(jnp.sum(spread * spread, axis=0) + smoothing * smoothing)


def double_layer(targets, sources, normals):
    spread = targets - sources
    distance = jnp.sum(spread * spread, axis=0) + smoothing * smoothing
    return inv_four_pi * jnp.sum(normals * spread, axis=0) / (distance * jnp.sqrt(distance))


def on_device(
    density,
    leaf_target,
    geometry,
    near_list,
    far_list,
    node_list,
    basis_in,
    basis_out,
    transfer,
    node_points,
):
    leaves, nrhs_here, leaf_size = density.shape
    rank_size = basis_in.shape[1]
    nodes_here = transfer.shape[0]
    children = leaves // nodes_here
    first_leaf = lax.axis_index(("row", "col")) * leaves
    zero_half = jnp.zeros((), jnp.bfloat16)
    destination = leaf_target // leaves
    tree_slot = leaf_target % leaves
    send_order = jnp.argsort(destination, stable=True)
    outgoing = density[send_order]
    out_slot = tree_slot[send_order]
    arrived, arrived_slot = (
        lax.all_to_all(outgoing, ("row", "col"), split_axis=0, concat_axis=0, tiled=True),
        lax.all_to_all(out_slot, ("row", "col"), split_axis=0, concat_axis=0, tiled=True),
    )
    ordered = arrived[jnp.argsort(arrived_slot)]
    geo_wide = extended(geometry, ((("row", "col"), 1),), REACH * leaf_size)
    shaped = geo_wide.reshape(6, leaves + 2 * REACH, leaf_size)
    proxies = shaped[0:3, :, :rank_size]
    skeleton = jnp.einsum(
        "tnl,trl->tnr", ordered, basis_in, preferred_element_type=jnp.float32
    ).astype(jnp.bfloat16)
    packed = jnp.concatenate(
        [
            ordered.reshape(leaves, nrhs_here * leaf_size),
            skeleton.reshape(leaves, nrhs_here * rank_size),
        ],
        axis=1,
    )
    packed_wide = extended(packed, ((("row", "col"), 0),), REACH)
    dens_wide = packed_wide[:, : nrhs_here * leaf_size].reshape(-1, nrhs_here, leaf_size)
    skel_wide = packed_wide[:, nrhs_here * leaf_size :].reshape(-1, nrhs_here, rank_size)
    local_ids = jnp.arange(leaves, dtype=jnp.int32) + REACH

    def near_block(packed_in):
        target_ids, entries = packed_in
        usable = entries >= 0
        sources = jnp.where(usable, entries - first_leaf + REACH, 0)
        source_geo = shaped[:, sources]
        kernel = double_layer(
            shaped[0:3, target_ids][:, :, None, :, None],
            source_geo[0:3][:, :, :, None, :],
            source_geo[3:6][:, :, :, None, :],
        ).astype(jnp.bfloat16)
        dens_src = jnp.where(usable[:, :, None, None], dens_wide[sources], zero_half)
        return jnp.einsum("bsij,bsnj->bni", kernel, dens_src, preferred_element_type=jnp.float32)

    per_step = 4
    near_out = lax.map(
        near_block,
        (local_ids.reshape(-1, per_step), near_list.reshape(-1, per_step, near_list.shape[1])),
    ).reshape(leaves, nrhs_here, leaf_size)

    def far_block(packed_in):
        target_ids, entries = packed_in
        usable = entries >= 0
        sources = jnp.where(usable, entries - first_leaf + REACH, 0)
        weights = coupling(
            proxies[:, target_ids][:, :, None, :, None], proxies[:, sources][:, :, :, None, :]
        ).astype(jnp.bfloat16)
        skel_src = jnp.where(usable[:, :, None, None], skel_wide[sources], zero_half)
        return jnp.einsum("bsij,bsnj->bni", weights, skel_src, preferred_element_type=jnp.float32)

    leaf_far = lax.map(
        far_block, (local_ids.reshape(-1, 16), far_list.reshape(-1, 16, far_list.shape[1]))
    ).reshape(leaves, nrhs_here, rank_size)
    stacked = (
        skeleton.reshape(nodes_here, children, nrhs_here, rank_size)
        .transpose(0, 2, 1, 3)
        .reshape(nodes_here, nrhs_here, children * rank_size)
    )
    node_skel = jnp.einsum(
        "pnk,prk->pnr", stacked, transfer, preferred_element_type=jnp.float32
    ).astype(jnp.bfloat16)
    all_skel = lax.all_gather(
        node_skel.reshape(nodes_here, nrhs_here * rank_size), ("row", "col"), axis=0, tiled=True
    ).reshape(-1, nrhs_here, rank_size)
    node_pts = node_points.reshape(3, -1, rank_size)
    my_nodes = first_leaf // children + jnp.arange(nodes_here, dtype=jnp.int32)
    usable = node_list >= 0
    sources = jnp.where(usable, node_list, 0)
    weights = coupling(
        node_pts[:, my_nodes][:, :, None, :, None], node_pts[:, sources][:, :, :, None, :]
    ).astype(jnp.bfloat16)
    skel_src = jnp.where(usable[:, :, None, None], all_skel[sources], zero_half)
    node_far = jnp.einsum(
        "bsij,bsnj->bni", weights, skel_src, preferred_element_type=jnp.float32
    ).astype(jnp.bfloat16)
    down = jnp.einsum("pnr,prk->pnk", node_far, transfer, preferred_element_type=jnp.float32)
    down = (
        down.reshape(nodes_here, nrhs_here, children, rank_size)
        .transpose(0, 2, 1, 3)
        .reshape(leaves, nrhs_here, rank_size)
    )
    local = (leaf_far + down).astype(jnp.bfloat16)
    far_out = jnp.einsum("tnr,trl->tnl", local, basis_out, preferred_element_type=jnp.float32)
    return (near_out + far_out).astype(jnp.bfloat16)


def solution(mesh):
    return jax.shard_map(
        on_device,
        mesh=mesh,
        in_specs=(
            P(("grp", "row", "col"), None, None),
            P(("grp", "row", "col")),
            P(None, ("grp", "row", "col")),
            P(("grp", "row", "col"), None),
            P(("grp", "row", "col"), None),
            P(("grp", "row", "col"), None),
            P(("grp", "row", "col"), None, None),
            P(("grp", "row", "col"), None, None),
            P(("grp", "row", "col"), None, None),
            P(None, "grp"),
        ),
        out_specs=P(("grp", "row", "col"), None, None),
        check_vma=False,
    )
```

profile of v0, /device:TPU:1, one launch (start us, length us, event | category | flops | bytes accessed | tf_op | source)
XLA Modules:
  0.0 249.2 jit_solution(13443230100099209576)
XLA Ops:
  0.1 0.7 and_select_fusion
  0.8 1.6 sort.34
  2.4 0.7 gather_fusion.7
  3.1 0.7 all_to_all.12
  3.8 7.3 %all-to-all-start.1 = ((s32[16,2,1]{1,2,0:T(1,128)}), s32[16,2,1]{1,2,0:T(1,128)S(1)}, u32[]{:S(2)}, u32[]{:S(2)}) async-start(s32[16,2,1]{1,2,0:T(1,128)} %bitcast.24), calls=%async_computation.1 | async-start | bytes 16384 | tf_op jit(solution)/shard_map/all_to_all | solution.py:68
  11.2 0.9 fusion.59
  12.0 2.0 collective-permute-start.3
  14.1 3.5 %collective-permute-start.2 = (f32[6,2048]{1,0:T(8,128)S(1)}, f32[6,2048]{1,0:T(8,128)S(1)}, u32[]{:S(2)}, u32[]{:S(2)}) collective-permute-start(f32[6,2048]{1,0:T(8,128)S(1)} %get-tuple-element.123), channel_id=1, source_target_pairs={{0,1},{1,2},{2,3},{3,4},{4,5},{5,6},{6,7},{7,8},{8,9},{9,10},{10,1... | collective-permute-start | bytes 147464 | tf_op jit(solution)/shard_map/ppermute | solution.py:23
  17.6 0.7 compare_select_fusion.4
  18.3 0.7 broadcast_compare_fusion
  19.0 1.0 reshape.245
  20.1 0.8 gather_fusion.11
  21.5 4.2 %multiply_reduce_fusion.1 = f32[4,32,64,64]{3,2,1,0:T(8,128)} fusion(f32[3,4,32,64]{3,2,1,0:T(8,128)S(1)} %copy.65, f32[3,4,64]{2,1,0:T(4,128)S(1)} %copy.63), kind=kLoop, calls=%fused_computation.56 | loop fusion | flops 4194304 | bytes 2198528 | tf_op jit(solution)/shard_map/reduce_sum | solution.py:34
  25.7 1.3 gather_fusion.6
  26.9 5.7 %all-to-all-start = ((bf16[32,32,128]{2,1,0:T(8,128)(2,1)}), bf16[32,32,128]{2,1,0:T(8,128)(2,1)S(1)}, u32[]{:S(2)}, u32[]{:S(2)}) async-start(bf16[32,32,128]{2,1,0:T(8,128)(2,1)} %gather_fusion.6), calls=%async_computation | async-start | bytes 524288 | tf_op jit(solution)/shard_map/all_to_all | solution.py:67
  33.4 0.7 reduce.3
  34.2 1.7 sort.35
  36.0 6.2 %all-to-all-done = bf16[32,32,128]{2,1,0:T(8,128)(2,1)S(1)} async-done(((bf16[32,32,128]{2,1,0:T(8,128)(2,1)}), bf16[32,32,128]{2,1,0:T(8,128)(2,1)S(1)}, u32[]{:S(2)}, u32[]{:S(2)}) %all-to-all-start) | async-done | bytes 262176 | tf_op jit(solution)/shard_map/all_to_all | solution.py:67
  43.6 0.8 fusion.58
  44.4 2.5 %collective-permute-start.1 = (bf16[16,6144]{1,0:T(8,128)(2,1)}, bf16[16,6144]{1,0:T(8,128)(2,1)}, u32[]{:S(2)}, u32[]{:S(2)}) collective-permute-start(bf16[16,6144]{1,0:T(8,128)(2,1)} %get-tuple-element.122), channel_id=1, source_target_pairs={{1,0},{2,1},{3,2},{4,3},{5,4},{6,5},{7,6},{8,7},{9,8},{10,9},{11,1... | collective-permute-start | bytes 589832 | tf_op jit(solution)/shard_map/ppermute | solution.py:25
  46.9 3.1 %collective-permute-start = (bf16[16,6144]{1,0:T(8,128)(2,1)}, bf16[16,6144]{1,0:T(8,128)(2,1)}, u32[]{:S(2)}, u32[]{:S(2)}) collective-permute-start(bf16[16,6144]{1,0:T(8,128)(2,1)} %get-tuple-element.121), channel_id=1, source_target_pairs={{0,1},{1,2},{2,3},{3,4},{4,5},{5,6},{6,7},{7,8},{8,9},{9,10},{10,1... | collective-permute-start | bytes 589832 | tf_op jit(solution)/shard_map/ppermute | solution.py:23
  50.6 19.2 %all-gather = bf16[16,4,2048]{2,1,0:T(4,128)(2,1)S(1)} all-gather(bf16[1,4,2048]{2,1,0:T(4,128)(2,1)S(1)} %reshape.353), channel_id=1, replica_groups=mesh['grp'=2,'row'=8,'col'=2] {'row','col'}, dimensions={0}, use_global_device_ids=true | all-gather | bytes 278528 | tf_op jit(solution)/shard_map/all_gather | solution.py:129
  70.2 0.8 gather_fusion.9
  70.9 3.1 %fusion.42 = f32[4,32,512]{2,1,0:T(8,128)S(1)} fusion(bf16[4,64,512]{2,1,0:T(8,128)(2,1)S(1)} %copy-done.1, f32[4,32,64,64]{3,2,1,0:T(8,128)} %multiply_reduce_fusion.1, bf16[4,32,32,64]{3,2,1,0:T(8,128)(2,1)S(1)} %bitcast.131, pred[4,32]{1,0:T(4,128)(4,1)S(1)} %broadcast_compare_fusion), kind=kOutput, calls=%fused_computation.67 | convolution fusion | flops 43786240 | bytes 3145856 | tf_op jit(solution)/shard_map/pnr,prk->pnk/dot_general | solution.py:143
  74.2 0.9 copy.66
  75.1 1.1 pad_maximum_fusion
  76.3 139.0 %while.20 = (s32[]{:T(128)}, f32[8,4,32,128]{3,2,1,0:T(8,128)S(1)}, s32[8,4,16]{2,1,0:T(4,128)S(1)}, s32[]{:T(128)}, bf16[64,32,128]{2,1,0:T(8,128)(2,1)S(1)}, /...) while((s32[]{:T(128)}, f32[8,4,32,128]{3,2,1,0:T(8,128)S(1)}, s32[8,4,16]{2,1,0:T(4,128)S(1)}, ...), condition=%wide.region_5.6_spmd, body=%wide.region_2.5_spmd.sunk | while | flops 86246872 | bytes 20210156 | solution.py:103
  78.0 9.8 %fusion.78 = (f32[4,16,128,128]{3,2,1,0:T(8,128)}, f32[4,16,128,128]{3,2,1,0:T(8,128)}) fusion(f32[3,4,16,128]{3,2,1,0:T(8,128)S(1)} %copy.78, f32[3,4,128]{2,1,0:T(4,128)S(1)} %bitcast.137, f32[3,4,16,128]{3,2,1,0:T(8,128)S(1)} %copy.80), kind=kLoop, calls=%fused_computation.14.clone.1 | loop fusion | flops 13631488 | bytes 8591360 | tf_op jit(solution)/shard_map/while/body/eval_jaxpr/reduce_sum | solution.py:40
  87.8 0.7 gather_fusion.2
  88.5 5.4 %fusion.79 = f32[8,4,32,128]{3,2,1,0:T(8,128)S(1)} fusion(f32[8,4,32,128]{3,2,1,0:T(8,128)S(1)} %get-tuple-element.240, s32[]{:T(128)S(6)} %copy.88, f32[4,16,128,128]{3,2,1,0:T(8,128)} %get-tuple-element.219, f32[4,16,128,128]{3,2,1,0:T(8,128)} %get-tuple-element.220, bf16[4,16,32,128]{3,2,1,0:T(8,128)(2,1)S(1)} %bitcast.130, ...), kind=kOutput, calls=%fused_computation.21.clone.1 | convolution fusion | flops 72613888 | bytes 8978948 | tf_op jit(solution)/shard_map/while/body/eval_jaxpr/bsij,bsnj->bni/dot_general | solution.py:100
  94.0 0.6 gather_fusion
  95.4 9.8 %fusion.78 = (f32[4,16,128,128]{3,2,1,0:T(8,128)}, f32[4,16,128,128]{3,2,1,0:T(8,128)}) fusion(f32[3,4,16,128]{3,2,1,0:T(8,128)S(1)} %copy.78, f32[3,4,128]{2,1,0:T(4,128)S(1)} %bitcast.137, f32[3,4,16,128]{3,2,1,0:T(8,128)S(1)} %copy.80), kind=kLoop, calls=%fused_computation.14.clone.1 | loop fusion | flops 13631488 | bytes 8591360 | tf_op jit(solution)/shard_map/while/body/eval_jaxpr/reduce_sum | solution.py:40
  105.2 0.7 gather_fusion.2
  105.9 5.4 %fusion.79 = f32[8,4,32,128]{3,2,1,0:T(8,128)S(1)} fusion(f32[8,4,32,128]{3,2,1,0:T(8,128)S(1)} %get-tuple-element.240, s32[]{:T(128)S(6)} %copy.88, f32[4,16,128,128]{3,2,1,0:T(8,128)} %get-tuple-element.219, f32[4,16,128,128]{3,2,1,0:T(8,128)} %get-tuple-element.220, bf16[4,16,32,128]{3,2,1,0:T(8,128)(2,1)S(1)} %bitcast.130, ...), kind=kOutput, calls=%fused_computation.21.clone.1 | convolution fusion | flops 72613888 | bytes 8978948 | tf_op jit(solution)/shard_map/while/body/eval_jaxpr/bsij,bsnj->bni/dot_general | solution.py:100
  112.7 9.8 %fusion.78 = (f32[4,16,128,128]{3,2,1,0:T(8,128)}, f32[4,16,128,128]{3,2,1,0:T(8,128)}) fusion(f32[3,4,16,128]{3,2,1,0:T(8,128)S(1)} %copy.78, f32[3,4,128]{2,1,0:T(4,128)S(1)} %bitcast.137, f32[3,4,16,128]{3,2,1,0:T(8,128)S(1)} %copy.80), kind=kLoop, calls=%fused_computation.14.clone.1 | loop fusion | flops 13631488 | bytes 8591360 | tf_op jit(solution)/shard_map/while/body/eval_jaxpr/reduce_sum | solution.py:40
  122.5 0.7 gather_fusion.2
  123.2 5.4 %fusion.79 = f32[8,4,32,128]{3,2,1,0:T(8,128)S(1)} fusion(f32[8,4,32,128]{3,2,1,0:T(8,128)S(1)} %get-tuple-element.240, s32[]{:T(128)S(6)} %copy.88, f32[4,16,128,128]{3,2,1,0:T(8,128)} %get-tuple-element.219, f32[4,16,128,128]{3,2,1,0:T(8,128)} %get-tuple-element.220, bf16[4,16,32,128]{3,2,1,0:T(8,128)(2,1)S(1)} %bitcast.130, ...), kind=kOutput, calls=%fused_computation.21.clone.1 | convolution fusion | flops 72613888 | bytes 8978948 | tf_op jit(solution)/shard_map/while/body/eval_jaxpr/bsij,bsnj->bni/dot_general | solution.py:100
  130.1 9.8 %fusion.78 = (f32[4,16,128,128]{3,2,1,0:T(8,128)}, f32[4,16,128,128]{3,2,1,0:T(8,128)}) fusion(f32[3,4,16,128]{3,2,1,0:T(8,128)S(1)} %copy.78, f32[3,4,128]{2,1,0:T(4,128)S(1)} %bitcast.137, f32[3,4,16,128]{3,2,1,0:T(8,128)S(1)} %copy.80), kind=kLoop, calls=%fused_computation.14.clone.1 | loop fusion | flops 13631488 | bytes 8591360 | tf_op jit(solution)/shard_map/while/body/eval_jaxpr/reduce_sum | solution.py:40
  139.9 0.7 gather_fusion.2
  140.6 5.4 %fusion.79 = f32[8,4,32,128]{3,2,1,0:T(8,128)S(1)} fusion(f32[8,4,32,128]{3,2,1,0:T(8,128)S(1)} %get-tuple-element.240, s32[]{:T(128)S(6)} %copy.88, f32[4,16,128,128]{3,2,1,0:T(8,128)} %get-tuple-element.219, f32[4,16,128,128]{3,2,1,0:T(8,128)} %get-tuple-element.220, bf16[4,16,32,128]{3,2,1,0:T(8,128)(2,1)S(1)} %bitcast.130, ...), kind=kOutput, calls=%fused_computation.21.clone.1 | convolution fusion | flops 72613888 | bytes 8978948 | tf_op jit(solution)/shard_map/while/body/eval_jaxpr/bsij,bsnj->bni/dot_general | solution.py:100
  147.4 9.8 %fusion.78 = (f32[4,16,128,128]{3,2,1,0:T(8,128)}, f32[4,16,128,128]{3,2,1,0:T(8,128)}) fusion(f32[3,4,16,128]{3,2,1,0:T(8,128)S(1)} %copy.78, f32[3,4,128]{2,1,0:T(4,128)S(1)} %bitcast.137, f32[3,4,16,128]{3,2,1,0:T(8,128)S(1)} %copy.80), kind=kLoop, calls=%fused_computation.14.clone.1 | loop fusion | flops 13631488 | bytes 8591360 | tf_op jit(solution)/shard_map/while/body/eval_jaxpr/reduce_sum | solution.py:40
  157.3 0.7 gather_fusion.2
  157.9 5.4 %fusion.79 = f32[8,4,32,128]{3,2,1,0:T(8,128)S(1)} fusion(f32[8,4,32,128]{3,2,1,0:T(8,128)S(1)} %get-tuple-element.240, s32[]{:T(128)S(6)} %copy.88, f32[4,16,128,128]{3,2,1,0:T(8,128)} %get-tuple-element.219, f32[4,16,128,128]{3,2,1,0:T(8,128)} %get-tuple-element.220, bf16[4,16,32,128]{3,2,1,0:T(8,128)(2,1)S(1)} %bitcast.130, ...), kind=kOutput, calls=%fused_computation.21.clone.1 | convolution fusion | flops 72613888 | bytes 8978948 | tf_op jit(solution)/shard_map/while/body/eval_jaxpr/bsij,bsnj->bni/dot_general | solution.py:100
  164.8 9.8 %fusion.78 = (f32[4,16,128,128]{3,2,1,0:T(8,128)}, f32[4,16,128,128]{3,2,1,0:T(8,128)}) fusion(f32[3,4,16,128]{3,2,1,0:T(8,128)S(1)} %copy.78, f32[3,4,128]{2,1,0:T(4,128)S(1)} %bitcast.137, f32[3,4,16,128]{3,2,1,0:T(8,128)S(1)} %copy.80), kind=kLoop, calls=%fused_computation.14.clone.1 | loop fusion | flops 13631488 | bytes 8591360 | tf_op jit(solution)/shard_map/while/body/eval_jaxpr/reduce_sum | solution.py:40
  174.6 0.7 gather_fusion.2
  175.3 5.4 %fusion.79 = f32[8,4,32,128]{3,2,1,0:T(8,128)S(1)} fusion(f32[8,4,32,128]{3,2,1,0:T(8,128)S(1)} %get-tuple-element.240, s32[]{:T(128)S(6)} %copy.88, f32[4,16,128,128]{3,2,1,0:T(8,128)} %get-tuple-element.219, f32[4,16,128,128]{3,2,1,0:T(8,128)} %get-tuple-element.220, bf16[4,16,32,128]{3,2,1,0:T(8,128)(2,1)S(1)} %bitcast.130, ...), kind=kOutput, calls=%fused_computation.21.clone.1 | convolution fusion | flops 72613888 | bytes 8978948 | tf_op jit(solution)/shard_map/while/body/eval_jaxpr/bsij,bsnj->bni/dot_general | solution.py:100
  182.2 9.8 %fusion.78 = (f32[4,16,128,128]{3,2,1,0:T(8,128)}, f32[4,16,128,128]{3,2,1,0:T(8,128)}) fusion(f32[3,4,16,128]{3,2,1,0:T(8,128)S(1)} %copy.78, f32[3,4,128]{2,1,0:T(4,128)S(1)} %bitcast.137, f32[3,4,16,128]{3,2,1,0:T(8,128)S(1)} %copy.80), kind=kLoop, calls=%fused_computation.14.clone.1 | loop fusion | flops 13631488 | bytes 8591360 | tf_op jit(solution)/shard_map/while/body/eval_jaxpr/reduce_sum | solution.py:40
  192.0 0.7 gather_fusion.2
  192.6 5.4 %fusion.79 = f32[8,4,32,128]{3,2,1,0:T(8,128)S(1)} fusion(f32[8,4,32,128]{3,2,1,0:T(8,128)S(1)} %get-tuple-element.240, s32[]{:T(128)S(6)} %copy.88, f32[4,16,128,128]{3,2,1,0:T(8,128)} %get-tuple-element.219, f32[4,16,128,128]{3,2,1,0:T(8,128)} %get-tuple-element.220, bf16[4,16,32,128]{3,2,1,0:T(8,128)(2,1)S(1)} %bitcast.130, ...), kind=kOutput, calls=%fused_computation.21.clone.1 | convolution fusion | flops 72613888 | bytes 8978948 | tf_op jit(solution)/shard_map/while/body/eval_jaxpr/bsij,bsnj->bni/dot_general | solution.py:100
  199.5 9.8 %fusion.78 = (f32[4,16,128,128]{3,2,1,0:T(8,128)}, f32[4,16,128,128]{3,2,1,0:T(8,128)}) fusion(f32[3,4,16,128]{3,2,1,0:T(8,128)S(1)} %copy.78, f32[3,4,128]{2,1,0:T(4,128)S(1)} %bitcast.137, f32[3,4,16,128]{3,2,1,0:T(8,128)S(1)} %copy.80), kind=kLoop, calls=%fused_computation.14.clone.1 | loop fusion | flops 13631488 | bytes 8591360 | tf_op jit(solution)/shard_map/while/body/eval_jaxpr/reduce_sum | solution.py:40
  209.3 0.7 gather_fusion.2
  210.0 5.4 %fusion.79 = f32[8,4,32,128]{3,2,1,0:T(8,128)S(1)} fusion(f32[8,4,32,128]{3,2,1,0:T(8,128)S(1)} %get-tuple-element.240, s32[]{:T(128)S(6)} %copy.88, f32[4,16,128,128]{3,2,1,0:T(8,128)} %get-tuple-element.219, f32[4,16,128,128]{3,2,1,0:T(8,128)} %get-tuple-element.220, bf16[4,16,32,128]{3,2,1,0:T(8,128)(2,1)S(1)} %bitcast.130, ...), kind=kOutput, calls=%fused_computation.21.clone.1 | convolution fusion | flops 72613888 | bytes 8978948 | tf_op jit(solution)/shard_map/while/body/eval_jaxpr/bsij,bsnj->bni/dot_general | solution.py:100
  215.4 1.0 pad_maximum_fusion.1
  217.0 28.9 %while.21 = (s32[]{:T(128)}, f32[2,16,32,64]{3,2,1,0:T(8,128)}, s32[2,16,16]{2,1,0:T(8,128)S(1)}, s32[]{:T(128)}, bf16[64,32,64]{2,1,0:T(8,128)(2,1)S(1)}, /*ind...) while((s32[]{:T(128)}, f32[2,16,32,64]{3,2,1,0:T(8,128)}, s32[2,16,16]{2,1,0:T(8,128)S(1)}, ...), condition=%wide.region_8.9_spmd, body=%wide.region_6.8_spmd.sunk | while | flops 79171376 | bytes 17051500 | solution.py:118
  217.1 1.0 gather_fusion.3
  218.8 6.6 %multiply_reduce_fusion.3 = f32[16,16,64,64]{3,2,1,0:T(8,128)} fusion(f32[3,16,16,64]{3,2,1,0:T(8,128)S(1)} %copy.81, f32[3,16,64]{2,1,0:T(8,128)S(1)} %copy.82), kind=kLoop, calls=%fused_computation.35.clone.1 | loop fusion | flops 8388608 | bytes 4403200 | tf_op jit(solution)/shard_map/while/body/eval_jaxpr/reduce_sum | solution.py:34
  225.4 1.0 gather_fusion.5
  226.4 5.0 %fusion.82 = f32[2,16,32,64]{3,2,1,0:T(8,128)} fusion(f32[2,16,32,64]{3,2,1,0:T(8,128)} %get-tuple-element.264, s32[]{:T(128)S(6)} %copy.94, f32[16,16,64,64]{3,2,1,0:T(8,128)} %multiply_reduce_fusion.3, bf16[16,16,32,64]{3,2,1,0:T(8,128)(2,1)S(1)} %bitcast.126, pred[16,16]{1,0:T(8,128)(4,1)S(1)} %bitcast.140), kind=kOutput, calls=%fused_computation.43.clone.1 | convolution fusion | flops 70778880 | bytes 9699588 | tf_op jit(solution)/shard_map/while/body/eval_jaxpr/bsij,bsnj->bni/dot_general | solution.py:116
  231.5 1.0 gather_fusion.3
  233.2 6.6 %multiply_reduce_fusion.3 = f32[16,16,64,64]{3,2,1,0:T(8,128)} fusion(f32[3,16,16,64]{3,2,1,0:T(8,128)S(1)} %copy.81, f32[3,16,64]{2,1,0:T(8,128)S(1)} %copy.82), kind=kLoop, calls=%fused_computation.35.clone.1 | loop fusion | flops 8388608 | bytes 4403200 | tf_op jit(solution)/shard_map/while/body/eval_jaxpr/reduce_sum | solution.py:34
  239.8 1.0 gather_fusion.5
  240.8 5.0 %fusion.82 = f32[2,16,32,64]{3,2,1,0:T(8,128)} fusion(f32[2,16,32,64]{3,2,1,0:T(8,128)} %get-tuple-element.264, s32[]{:T(128)S(6)} %copy.94, f32[16,16,64,64]{3,2,1,0:T(8,128)} %multiply_reduce_fusion.3, bf16[16,16,32,64]{3,2,1,0:T(8,128)(2,1)S(1)} %bitcast.126, pred[16,16]{1,0:T(8,128)(4,1)S(1)} %bitcast.140), kind=kOutput, calls=%fused_computation.43.clone.1 | convolution fusion | flops 70778880 | bytes 9699588 | tf_op jit(solution)/shard_map/while/body/eval_jaxpr/bsij,bsnj->bni/dot_general | solution.py:116
  245.9 1.3 fusion.47
  247.2 2.0 fusion.39
  (155 shorter events, 17.2 us)
Async XLA Ops:
  0.0 247.2 %copy-start = (bf16[32,64,128]{2,1,0:T(8,128)(2,1)S(1)}, bf16[32,64,128]{2,1,0:T(8,128)(2,1)}, u32[]{:S(2)}) copy-start(bf16[32,64,128]{2,1,0:T(8,128)(2,1)} %param.21) | copy-start | bytes 1572868
  0.0 35.9 %copy-start.5 = (f32[6,4096]{1,0:T(8,128)S(1)}, f32[6,4096]{1,0:T(8,128)}, u32[]{:S(2)}) copy-start(f32[6,4096]{1,0:T(8,128)} %param.16) | copy-start | bytes 294916
  0.0 25.6 %copy-start.6 = (bf16[32,32,128]{2,1,0:T(8,128)(2,1)S(1)}, bf16[32,32,128]{2,1,0:T(8,128)(2,1)}, u32[]{:S(2)}) copy-start(bf16[32,32,128]{2,1,0:T(8,128)(2,1)} %param.14) | copy-start | bytes 786436
  0.0 32.7 %copy-start.7 = (s32[32,16]{0,1:T(8,128)S(1)}, s32[32,16]{0,1:T(8,128)}, u32[]{:S(2)}) copy-start(s32[32,16]{0,1:T(8,128)} %param.17) | copy-start | bytes 6148
  0.0 32.8 %copy-start.8 = (s32[32,16]{0,1:T(8,128)S(1)}, s32[32,16]{0,1:T(8,128)}, u32[]{:S(2)}) copy-start(s32[32,16]{0,1:T(8,128)} %param.18) | copy-start | bytes 6148
  3.8 23.1 %all-to-all-start.1 = ((s32[16,2,1]{1,2,0:T(1,128)}), s32[16,2,1]{1,2,0:T(1,128)S(1)}, u32[]{:S(2)}, u32[]{:S(2)}) async-start(s32[16,2,1]{1,2,0:T(1,128)} %bitcast.24), calls=%async_computation.1 | async-start | bytes 16384 | tf_op jit(solution)/shard_map/all_to_all | solution.py:68
  12.0 23.8 %collective-permute-start.3 = (f32[6,2048]{1,0:T(8,128)S(1)}, f32[6,2048]{1,0:T(8,128)S(1)}, u32[]{:S(2)}, u32[]{:S(2)}) collective-permute-start(f32[6,2048]{1,0:T(8,128)S(1)} %get-tuple-element.124), channel_id=1, source_target_pairs={{1,0},{2,1},{3,2},{4,3},{5,4},{6,5},{7,6},{8,7},{9,8},{10,9},{11,1... | collective-permute-start | bytes 147464 | tf_op jit(solution)/shard_map/ppermute | solution.py:25
  14.1 21.8 %collective-permute-start.2 = (f32[6,2048]{1,0:T(8,128)S(1)}, f32[6,2048]{1,0:T(8,128)S(1)}, u32[]{:S(2)}, u32[]{:S(2)}) collective-permute-start(f32[6,2048]{1,0:T(8,128)S(1)} %get-tuple-element.123), channel_id=1, source_target_pairs={{0,1},{1,2},{2,3},{3,4},{4,5},{5,6},{6,7},{7,8},{8,9},{9,10},{10,1... | collective-permute-start | bytes 147464 | tf_op jit(solution)/shard_map/ppermute | solution.py:23
  20.0 22.9 %copy-start.4 = (bf16[32,64,128]{2,1,0:T(8,128)(2,1)S(1)}, bf16[32,64,128]{2,1,0:T(8,128)(2,1)}, u32[]{:S(2)}) copy-start(bf16[32,64,128]{2,1,0:T(8,128)(2,1)} %param.20) | copy-start | bytes 1572868
  25.6 24.6 %copy-start.1 = (bf16[4,64,512]{2,1,0:T(8,128)(2,1)S(1)}, bf16[4,64,512]{2,1,0:T(8,128)(2,1)}, u32[]{:S(2)}) copy-start(bf16[4,64,512]{2,1,0:T(8,128)(2,1)} %param.22) | copy-start | bytes 786436
  26.9 15.3 %all-to-all-start = ((bf16[32,32,128]{2,1,0:T(8,128)(2,1)}), bf16[32,32,128]{2,1,0:T(8,128)(2,1)S(1)}, u32[]{:S(2)}, u32[]{:S(2)}) async-start(bf16[32,32,128]{2,1,0:T(8,128)(2,1)} %gather_fusion.6), calls=%async_computation | async-start | bytes 524288 | tf_op jit(solution)/shard_map/all_to_all | solution.py:67
  44.4 30.7 %collective-permute-start.1 = (bf16[16,6144]{1,0:T(8,128)(2,1)}, bf16[16,6144]{1,0:T(8,128)(2,1)}, u32[]{:S(2)}, u32[]{:S(2)}) collective-permute-start(bf16[16,6144]{1,0:T(8,128)(2,1)} %get-tuple-element.122), channel_id=1, source_target_pairs={{1,0},{2,1},{3,2},{4,3},{5,4},{6,5},{7,6},{8,7},{9,8},{10,9},{11,1... | collective-permute-start | bytes 589832 | tf_op jit(solution)/shard_map/ppermute | solution.py:25
  46.9 28.2 %collective-permute-start = (bf16[16,6144]{1,0:T(8,128)(2,1)}, bf16[16,6144]{1,0:T(8,128)(2,1)}, u32[]{:S(2)}, u32[]{:S(2)}) collective-permute-start(bf16[16,6144]{1,0:T(8,128)(2,1)} %get-tuple-element.121), channel_id=1, source_target_pairs={{0,1},{1,2},{2,3},{3,4},{4,5},{5,6},{6,7},{7,8},{8,9},{9,10},{10,1... | collective-permute-start | bytes 589832 | tf_op jit(solution)/shard_map/ppermute | solution.py:23
  74.0 2.3 copy-start.2
  215.4 1.6 copy-start.3
where the time goes:
time: 250 us; the launch traced here: 249 us
  other arithmetic  106 us (42%)
  matrix products  58.9 us (24%)
  local copies, waits for them, and re-layouts  33.7 us (13%)
  starting transfers between devices  24.2 us (10%)
  blocking collectives  19.2 us (8%)
  waiting for transfers between devices  6.26 us (3%)
    reduce_sum x8, other arithmetic, double_layer(): jnp.sum(normals * spread, axis=0)  78.5 us
    dot_general x8, matrix products, near_block(): jnp.einsum('bsij,bsnj->bni', kernel, dens_src, preferred_element_type=jnp...  43.2 us
    all_gather x1, blocking collectives, on_device(): lax.all_gather(node_skel.reshape(nodes_here, nrhs_here * rank_size), ('ro...  19.2 us
    reduce_sum x3, other arithmetic, coupling(): jnp.sum(spread * spread, axis=0) + smoothing * smoothing  17.4 us
    dot_general x2, matrix products, far_block(): jnp.einsum('bsij,bsnj->bni', weights, skel_src, preferred_element_type=jn...  10.1 us
    all_to_all x1, starting transfers between devices, on_device(): lax.all_to_all(out_slot, ('row', 'col'), split_axis=0, concat_axis=0, til...  7.34 us
    ppermute x2, starting transfers between devices, extended(): lax.ppermute(tail, axis, [(i, (i + 1) % count) for i in range(ends)])  6.61 us
    all_to_all x1, waiting for transfers between devices, on_device(): lax.all_to_all(outgoing, ('row', 'col'), split_axis=0, concat_axis=0, til...  6.24 us
  transfers between devices with their start and end apart: 6, of which 1 were waited for; matrix products, arithmetic and copies ran while one was open for 8% of the time, Pallas kernels for 0%

commit v1 on v0

v1 whole, which is shorter than its diff:
```python
import functools
import math

import jax
import jax.numpy as jnp
from jax import lax
from jax.experimental import pallas as pl
from jax.experimental.pallas import tpu as pltpu
from jax.sharding import PartitionSpec as P

REACH = 16
smoothing = 0.1
inv_four_pi = 0.25 / math.pi
NT = (((1,), (1,)), ((), ()))


def extended(cells, sides, width):
    for axis, dim in sides:
        count = lax.axis_size(axis)
        ends = count - 1
        head = lax.slice_in_dim(cells, 0, width, axis=dim)
        tail = lax.slice_in_dim(cells, cells.shape[dim] - width, cells.shape[dim], axis=dim)
        cells = jnp.concatenate(
            [
                lax.ppermute(tail, axis, [(i, (i + 1) % count) for i in range(ends)]),
                cells,
                lax.ppermute(head, axis, [((i + 1) % count, i) for i in range(ends)]),
            ],
            axis=dim,
        )
    return cells


def compacted(entries, base, pad):
    live = entries >= 0
    place = jnp.cumsum(live.astype(jnp.int32), axis=1) - 1
    slots = jnp.arange(entries.shape[1], dtype=jnp.int32)
    hit = live[:, :, None] & (place[:, :, None] == slots)
    return (
        jnp.max(jnp.where(hit, (entries + base)[:, :, None], -1), axis=1),
        pad,
        jnp.sum(live.astype(jnp.int32), axis=1),
    )


def fill(packed):
    rows, pad, count = packed
    return jnp.where(rows < 0, pad, rows), count


def thirds(a):
    high = a.astype(jnp.bfloat16).astype(jnp.float32)
    rest = a - high
    mid = rest.astype(jnp.bfloat16).astype(jnp.float32)
    return high, mid, rest - mid


def left_side(a):
    h, m, l = thirds(a)
    return jnp.concatenate([h, m, h, l, h, m], axis=0)


def right_side(a):
    h, m, l = thirds(a)
    return jnp.concatenate([h, h, m, h, l, m], axis=0)


def point_forms(points, row):
    xyz = jnp.where(row < 3, points, 0.0)
    square = jnp.sum(xyz * xyz, axis=0, keepdims=True)
    target = jnp.where(row < 3, points, jnp.where(row == 3, square, jnp.where(row == 4, 1.0, 0.0)))
    source = jnp.where(
        row < 3,
        -2.0 * points,
        jnp.where(row == 3, 1.0, jnp.where(row == 4, square + smoothing * smoothing, 0.0)),
    )
    return xyz, target, source


def halves(a, lane):
    return jnp.where(lane < 64, a, 0.0), jnp.where(lane < 64, 0.0, pltpu.roll(a, 64, 1))


def field_kernel(
    wide, nodes, chunk,
    near_idx, near_cnt, far_idx, far_cnt, node_idx, node_cnt, first_node,
    geo, dens, skel, node_pts, node_skel, transfer, basis_out, out,
    target_form, source_form, far_form, far_skel, node_target, node_form, node_dens, down,
):
    leaves, nrhs, leaf_size = out.shape
    nodes_here, rank, width = transfer.shape
    children = width // rank
    bf16, f32 = jnp.bfloat16, jnp.float32
    row = lax.broadcasted_iota(jnp.int32, (8, leaf_size), 0)
    lane = lax.broadcasted_iota(jnp.int32, (1, leaf_size), 1)
    low = lane < rank

    def columns(ref, block):
        return ref[:, pl.ds(pl.multiple_of(block * leaf_size, leaf_size), leaf_size)]

    def node_block(b, carry):
        _, _, source = point_forms(columns(node_pts, b), row)
        form = right_side(source)
        turned = pltpu.roll(form, rank, 1)
        node_form[0, 2 * b] = jnp.where(low, form, 0.0).astype(bf16)
        node_form[1, 2 * b] = jnp.where(low, 0.0, turned).astype(bf16)
        node_form[0, 2 * b + 1] = jnp.where(low, turned, 0.0).astype(bf16)
        node_form[1, 2 * b + 1] = jnp.where(low, 0.0, form).astype(bf16)
        return carry

    lax.fori_loop(0, nodes // 2, node_block, 0)
    node_form[0, nodes] = node_form[0, 0]
    node_form[1, nodes] = node_form[1, 0]

    def spread(skel_ref, spread_ref, count):
        def step(s, carry):
            both = jnp.concatenate([skel_ref[s], skel_ref[s]], axis=1)
            none = jnp.zeros_like(both)
            spread_ref[0, s] = jnp.where(low, both, none)
            spread_ref[1, s] = jnp.where(low, none, both)
            return carry

        lax.fori_loop(0, count, step, 0)
        spread_ref[0, count] = jnp.zeros((nrhs, leaf_size), bf16)
        spread_ref[1, count] = jnp.zeros((nrhs, leaf_size), bf16)

    spread(node_skel, node_dens, nodes)
    spread(skel, far_skel, wide)

    for b in range(nodes_here // 2):
        _, target, _ = point_forms(columns(node_pts, first_node[0] // 2 + b), row)
        turned = left_side(target).T.astype(bf16)
        node_target[2 * b] = turned[:rank]
        node_target[2 * b + 1] = turned[rank:]

    def leaf_block(s, carry):
        points = columns(geo, s)
        xyz, target, source = point_forms(points, row)
        normal = jnp.where(row < 3, pltpu.roll(points, 5, 0), 0.0) * inv_four_pi
        shift = -jnp.sum(normal * xyz, axis=0, keepdims=True)
        normal = jnp.where(row == 4, shift, normal)
        form = right_side(source)
        source_form[s] = jnp.concatenate([form, right_side(normal)], axis=1).astype(bf16)
        far_form[0, s] = jnp.where(low, form, 0.0).astype(bf16)
        far_form[1, s] = jnp.where(low, 0.0, pltpu.roll(form, rank, 1)).astype(bf16)
        return carry

    lax.fori_loop(0, wide, leaf_block, 0)
    source_form[wide] = source_form[0]
    far_form[0, wide] = far_form[0, 0]
    far_form[1, wide] = far_form[1, 0]

    def own_block(t, carry):
        _, target, _ = point_forms(columns(geo, t + REACH), row)
        target_form[t] = left_side(target).T.astype(bf16)
        return carry

    lax.fori_loop(0, leaves, own_block, 0)

    def coupled(idx, count, t, form, points, charges):
        def step(c, acc):
            ids = [idx[t, c * chunk + k] for k in range(chunk)]
            weights = jnp.concatenate(
                [points[0, ids[k]] + points[1, ids[k + 1]] for k in range(0, chunk, 2)], axis=1
            )
            square = jnp.dot(form, weights, preferred_element_type=f32)
            kernel = (inv_four_pi * lax.rsqrt(square)).astype(bf16)
            charge = jnp.concatenate(
                [charges[0, ids[k]] + charges[1, ids[k + 1]] for k in range(0, chunk, 2)], axis=1
            )
            return acc + lax.dot_general(charge, kernel, NT, preferred_element_type=f32)

        return lax.fori_loop(0, (count[t] + chunk - 1) // chunk, step, jnp.zeros((nrhs, rank), f32))

    for p in range(nodes_here):
        far = coupled(node_idx, node_cnt, p, node_target[p], node_form, node_dens).astype(bf16)
        spreading = jnp.dot(far, transfer[p], preferred_element_type=f32)
        for c in range(children):
            down[p * children + c] = spreading[:, c * rank : (c + 1) * rank]

    def leaf(t, carry):
        form = target_form[t]
        far = coupled(far_idx, far_cnt, t, form[:rank], far_form, far_skel)
        local = (far + down[t]).astype(bf16)
        start = jnp.dot(local, basis_out[t], preferred_element_type=f32)

        def step(c, acc):
            kernels, charges = [], []
            for k in range(chunk):
                s = near_idx[t, c * chunk + k]
                both = jnp.dot(form, source_form[s], preferred_element_type=f32)
                r = lax.rsqrt(both[:, :leaf_size])
                kernels.append((both[:, leaf_size:] * (r * r * r)).astype(bf16))
                charges.append(dens[s])
            return acc + lax.dot_general(
                jnp.concatenate(charges, axis=1),
                jnp.concatenate(kernels, axis=1),
                NT,
                preferred_element_type=f32,
            )

        out[t] = lax.fori_loop(0, (near_cnt[t] + chunk - 1) // chunk, step, start).astype(bf16)
        return carry

    lax.fori_loop(0, leaves, leaf, 0)


def field(near, far, node, first_node, geo, dens, skel, node_pts, node_skel, transfer, basis_out):
    wide, nodes = skel.shape[0], node_skel.shape[0]
    nrhs, leaf_size = dens.shape[1:]
    nodes_here, rank, width = transfer.shape
    leaves = basis_out.shape[0]
    terms = 48
    bf16 = jnp.bfloat16
    smem = pl.BlockSpec(memory_space=pltpu.SMEM)
    vmem = pl.BlockSpec(memory_space=pltpu.VMEM)
    return pl.pallas_call(
        functools.partial(field_kernel, wide, nodes, 4),
        out_shape=jax.ShapeDtypeStruct((leaves, nrhs, leaf_size), bf16),
        in_specs=[smem] * 7 + [vmem] * 7,
        out_specs=vmem,
        scratch_shapes=[
            pltpu.VMEM((leaves, leaf_size, terms), bf16),
            pltpu.VMEM((wide + 1, terms, 2 * leaf_size), bf16),
            pltpu.VMEM((2, wide + 1, terms, leaf_size), bf16),
            pltpu.VMEM((2, wide + 1, nrhs, leaf_size), bf16),
            pltpu.VMEM((nodes_here, rank, terms), bf16),
            pltpu.VMEM((2, nodes + 1, terms, leaf_size), bf16),
            pltpu.VMEM((2, nodes + 1, nrhs, leaf_size), bf16),
            pltpu.VMEM((leaves, nrhs, rank), jnp.float32),
        ],
        compiler_params=pltpu.CompilerParams(vmem_limit_bytes=48 * 1024 * 1024),
        name="field",
    )(*near, *far, *node, first_node, geo, dens, skel, node_pts, node_skel, transfer, basis_out)


def on_device(
    density,
    leaf_target,
    geometry,
    near_list,
    far_list,
    node_list,
    basis_in,
    basis_out,
    transfer,
    node_points,
):
    leaves, nrhs_here, leaf_size = density.shape
    rank_size = basis_in.shape[1]
    nodes_here = transfer.shape[0]
    children = leaves // nodes_here
    wide = leaves + 2 * REACH
    first_leaf = lax.axis_index(("row", "col")) * leaves
    destination = leaf_target // leaves
    tree_slot = leaf_target % leaves
    send_order = jnp.argsort(destination, stable=True)
    outgoing = density[send_order]
    out_slot = tree_slot[send_order]
    arrived, arrived_slot = (
        lax.all_to_all(outgoing, ("row", "col"), split_axis=0, concat_axis=0, tiled=True),
        lax.all_to_all(out_slot, ("row", "col"), split_axis=0, concat_axis=0, tiled=True),
    )
    ordered = arrived[jnp.argsort(arrived_slot)]
    geo_wide = extended(
        jnp.pad(geometry, ((0, 2), (0, 0))), ((("row", "col"), 1),), REACH * leaf_size
    )
    skeleton = jnp.einsum(
        "tnl,trl->tnr", ordered, basis_in, preferred_element_type=jnp.float32
    ).astype(jnp.bfloat16)
    dens_wide = extended(ordered, ((("row", "col"), 0),), REACH)
    dens_wide = jnp.pad(dens_wide, ((0, 1), (0, 0), (0, 0)))
    skel_wide = extended(skeleton, ((("row", "col"), 0),), REACH)
    stacked = (
        skeleton.reshape(nodes_here, children, nrhs_here, rank_size)
        .transpose(0, 2, 1, 3)
        .reshape(nodes_here, nrhs_here, children * rank_size)
    )
    node_skel = jnp.einsum(
        "pnk,prk->pnr", stacked, transfer, preferred_element_type=jnp.float32
    ).astype(jnp.bfloat16)
    all_skel = lax.all_gather(
        node_skel.reshape(nodes_here, nrhs_here * rank_size), ("row", "col"), axis=0, tiled=True
    ).reshape(-1, nrhs_here, rank_size)
    nodes = all_skel.shape[0]
    near = fill(compacted(near_list, REACH - first_leaf, wide))
    far = fill(compacted(far_list, REACH - first_leaf, wide))
    node = fill(compacted(node_list, 0, nodes))
    first_node = (first_leaf // children).reshape(1)
    node_pts = jnp.pad(node_points, ((0, 5), (0, 0)))
    return field(
        near, far, node, first_node, geo_wide, dens_wide, skel_wide, node_pts, all_skel,
        transfer, basis_out,
    )


def solution(mesh):
    return jax.shard_map(
        on_device,
        mesh=mesh,
        in_specs=(
            P(("grp", "row", "col"), None, None),
            P(("grp", "row", "col")),
            P(None, ("grp", "row", "col")),
            P(("grp", "row", "col"), None),
            P(("grp", "row", "col"), None),
            P(("grp", "row", "col"), None),
            P(("grp", "row", "col"), None, None),
            P(("grp", "row", "col"), None, None),
            P(("grp", "row", "col"), None, None),
            P(None, "grp"),
        ),
        out_specs=P(("grp", "row", "col"), None, None),
        check_vma=False,
    )
```

time: 250 us -> 171 us (0.68)
  other arithmetic: 106 us -> 6.9 us
  Pallas kernels: 0 us -> 97.7 us
  matrix products: 58.9 us -> 0.55 us
  local copies, waits for them, and re-layouts: 33.7 us -> 6.52 us
  starting transfers between devices: 24.2 us -> 28.5 us
    pallas_call x0 -> x1, Pallas kernels: none -> 97.7 us  [field(): pl.pallas_call(functools.partial(field_kernel, wide, nodes, 4), out_shape...]
    reduce_sum x11 -> x2, other arithmetic: 95.9 us -> 0.23 us  [compacted(): jnp.sum(live.astype(jnp.int32), axis=1)]
    dot_general x12 -> x0, matrix products: 58.3 us -> none  [the longest x8 43.2 us: near_block(): jnp.einsum('bsij,bsnj->bni', kernel, dens_src, preferred_element_type=jnp...]
    gather x39 -> x0, local copies, waits for them, and re-layouts: 22.2 us -> none  [the longest x8 5.22 us: near_block(): dens_wide[sources]]
    ppermute x2 -> x3, starting transfers between devices: 6.61 us -> 8.75 us  [extended(): lax.ppermute(tail, axis, [(i, (i + 1) % count) for i in range(ends)])]
    ppermute x2 -> x3, starting transfers between devices: 4.51 us -> 6.25 us  [extended(): lax.ppermute(head, axis, [((i + 1) % count, i) for i in range(ends)])]
  transfers between devices with their start and end apart: 6 -> 8, of which waited for: 1 -> 1; matrix products, arithmetic and copies ran while one was open for 8% -> 5% of each run, Pallas kernels for 0% -> 0%
where the time goes in v1:
time: 171 us; the launch traced here: 168 us
  Pallas kernels  97.7 us (57%)
  starting transfers between devices  28.5 us (17%)
  blocking collectives  21.5 us (13%)
  other arithmetic  6.9 us (4%)
  local copies, waits for them, and re-layouts  6.52 us (4%)
  waiting for transfers between devices  6.38 us (4%)
    pallas_call x1, Pallas kernels, field(): pl.pallas_call(functools.partial(field_kernel, wide, nodes, 4), out_shape...  97.7 us
    all_gather x1, blocking collectives, on_device(): lax.all_gather(node_skel.reshape(nodes_here, nrhs_here * rank_size), ('ro...  21.5 us
    ppermute x3, starting transfers between devices, extended(): lax.ppermute(tail, axis, [(i, (i + 1) % count) for i in range(ends)])  8.75 us
    all_to_all x1, starting transfers between devices, on_device(): lax.all_to_all(out_slot, ('row', 'col'), split_axis=0, concat_axis=0, til...  7.34 us
    all_to_all x1, waiting for transfers between devices, on_device(): lax.all_to_all(outgoing, ('row', 'col'), split_axis=0, concat_axis=0, til...  6.36 us
    ppermute x3, starting transfers between devices, extended(): lax.ppermute(head, axis, [((i + 1) % count, i) for i in range(ends)])  6.25 us
    all_to_all x1, starting transfers between devices, on_device(): lax.all_to_all(outgoing, ('row', 'col'), split_axis=0, concat_axis=0, til...  6.13 us
  transfers between devices with their start and end apart: 8, of which 1 were waited for; matrix products, arithmetic and copies ran while one was open for 5% of the time, Pallas kernels for 0%

profile of v1, /device:TPU:1, one launch (start us, length us, event | category | flops | bytes accessed | tf_op | source)
XLA Modules:
  0.0 168.3 jit_solution(9284198517650826639)
XLA Ops:
  0.0 0.0 copy-start
  0.0 0.0 copy-start.6
  0.0 0.0 copy-start.4
  0.0 0.7 and_select_fusion
  0.8 1.6 sort.34
  2.4 0.7 gather_fusion.1
  3.1 0.7 all_to_all.12
  3.8 7.3 %all-to-all-start.1 = ((s32[16,2,1]{1,2,0:T(1,128)}), s32[16,2,1]{1,2,0:T(1,128)S(1)}, u32[]{:S(2)}, u32[]{:S(2)}) async-start(s32[16,2,1]{1,2,0:T(1,128)} %bitcast.1), calls=%async_computation.1 | async-start | bytes 16384 | tf_op jit(solution)/shard_map/all_to_all | solution.py:262
  11.1 0.0 copy-done.3
  11.1 3.5 %collective-permute-start = (f32[8,2048]{1,0:T(8,128)S(1)}, f32[8,2048]{1,0:T(8,128)S(1)}, u32[]{:S(2)}, u32[]{:S(2)}) collective-permute-start(f32[8,2048]{1,0:T(8,128)S(1)} %get-tuple-element.19), channel_id=1, source_target_pairs={{0,1},{1,2},{2,3},{3,4},{4,5},{5,6},{6,7},{7,8},{8,9},{9,10},{10,1... | collective-permute-start | bytes 196616 | tf_op jit(solution)/shard_map/ppermute | solution.py:25
  14.7 1.9 %collective-permute-start.1 = (f32[8,2048]{1,0:T(8,128)S(1)}, f32[8,2048]{1,0:T(8,128)S(1)}, u32[]{:S(2)}, u32[]{:S(2)}) collective-permute-start(f32[8,2048]{1,0:T(8,128)S(1)} %get-tuple-element.20), channel_id=1, source_target_pairs={{1,0},{2,1},{3,2},{4,3},{5,4},{6,5},{7,6},{8,7},{9,8},{10,9},{11,1... | collective-permute-start | bytes 196616 | tf_op jit(solution)/shard_map/ppermute | solution.py:27
  16.6 0.0 copy-done.7
  16.6 0.1 copy.27
  16.7 0.0 copy-done.6
  16.7 0.1 copy.32
  16.8 0.1 convert_reduce_fusion
  16.9 0.1 copy.33
  17.0 0.1 copy.28
  17.1 0.0 copy-done.4
  17.1 0.0 copy-start.5
  17.1 1.3 gather_fusion
  18.4 0.2 reduce_window_sum.29
  18.6 0.1 copy.34
  18.7 0.1 copy.35
  18.8 0.2 reduce_window_sum.28
  19.0 0.1 copy.29
  19.0 0.1 select_reduce_fusion.1
  19.1 0.1 copy.30
  19.2 0.0 copy-done.8
  19.2 0.1 convert_reduce_fusion.2
  19.3 0.2 reduce_window_sum.30
  19.5 0.1 select_reduce_fusion.2
  19.7 0.0 copy-done.5
  19.7 0.0 all-to-all-done.1
  19.7 6.1 %all-to-all-start = ((bf16[32,32,128]{2,1,0:T(8,128)(2,1)}), bf16[32,32,128]{2,1,0:T(8,128)(2,1)S(1)}, u32[]{:S(2)}, u32[]{:S(2)}) async-start(bf16[32,32,128]{2,1,0:T(8,128)(2,1)} %gather_fusion), calls=%async_computation | async-start | bytes 524288 | tf_op jit(solution)/shard_map/all_to_all | solution.py:261
  25.9 0.6 broadcast.105
  26.5 0.7 reduce.3
  27.2 0.1 all_to_all.14
  27.3 1.7 %sort.35 = (s32[32]{0:T(128)}, s32[32]{0:T(128)S(1)}) sort(s32[32]{0:T(128)S(1)} %all_to_all.14, s32[32]{0:T(128)S(1)} %iota.18), dimensions={0}, to_apply=%region_10.11 | sort | flops 160 | bytes 512 | tf_op jit(solution)/shard_map/jit(argsort)/sort | solution.py:264
  29.0 0.0 collective-permute-done
  29.0 0.0 collective-permute-done.1
  29.0 6.4 %all-to-all-done = bf16[32,32,128]{2,1,0:T(8,128)(2,1)S(1)} async-done(((bf16[32,32,128]{2,1,0:T(8,128)(2,1)}), bf16[32,32,128]{2,1,0:T(8,128)(2,1)S(1)}, u32[]{:S(2)}, u32[]{:S(2)}) %all-to-all-start) | async-done | bytes 262176 | tf_op jit(solution)/shard_map/all_to_all | solution.py:261
  35.4 0.6 gather_fusion.2
  36.0 0.4 convolution_convert_fusion
  36.4 0.0 copy-start.1
  36.5 2.1 %collective-permute-start.4 = (bf16[16,32,64]{2,1,0:T(8,128)(2,1)S(1)}, bf16[16,32,64]{2,1,0:T(8,128)(2,1)S(1)}, u32[]{:S(2)}, u32[]{:S(2)}) collective-permute-start(bf16[16,32,64]{2,1,0:T(8,128)(2,1)S(1)} %get-tuple-element.15), channel_id=1, source_target_pairs={{0,1},{1,2},{2,3},{3,4},{4,5},{5,6},{6,7},{7,8},{8,9},{9,10},{10,1... | collective-permute-start | bytes 196616 | tf_op jit(solution)/shard_map/ppermute | solution.py:25
  38.5 2.4 %collective-permute-start.5 = (bf16[16,32,64]{2,1,0:T(8,128)(2,1)S(1)}, bf16[16,32,64]{2,1,0:T(8,128)(2,1)}, u32[]{:S(2)}, u32[]{:S(2)}) collective-permute-start(bf16[16,32,64]{2,1,0:T(8,128)(2,1)S(1)} %get-tuple-element.16), channel_id=1, source_target_pairs={{1,0},{2,1},{3,2},{4,3},{5,4},{6,5},{7,6},{8,7},{9,8},{10,9},{11,1... | collective-permute-start | bytes 196616 | tf_op jit(solution)/shard_map/ppermute | solution.py:27
  40.9 3.2 %collective-permute-start.2 = (bf16[16,32,128]{2,1,0:T(8,128)(2,1)S(1)}, bf16[16,32,128]{2,1,0:T(8,128)(2,1)S(1)}, u32[]{:S(2)}, u32[]{:S(2)}) collective-permute-start(bf16[16,32,128]{2,1,0:T(8,128)(2,1)S(1)} %get-tuple-element.17), channel_id=1, source_target_pairs={{0,1},{1,2},{2,3},{3,4},{4,5},{5,6},{6,7},{7,8},{8,9},{9,10},{10,1... | collective-permute-start | bytes 393224 | tf_op jit(solution)/shard_map/ppermute | solution.py:25
  44.1 1.9 %collective-permute-start.3 = (bf16[16,32,128]{2,1,0:T(8,128)(2,1)S(1)}, bf16[16,32,128]{2,1,0:T(8,128)(2,1)S(1)}, u32[]{:S(2)}, u32[]{:S(2)}) collective-permute-start(bf16[16,32,128]{2,1,0:T(8,128)(2,1)S(1)} %get-tuple-element.18), channel_id=1, source_target_pairs={{1,0},{2,1},{3,2},{4,3},{5,4},{6,5},{7,6},{8,7},{9,8},{10,9},{11,1... | collective-permute-start | bytes 393224 | tf_op jit(solution)/shard_map/ppermute | solution.py:27
  46.0 0.1 copy.38
  46.1 0.2 reshape.46
  46.3 0.0 copy-done.1
  46.4 0.2 convolution_convert_fusion.1
  46.5 0.1 reshape.76
  46.7 21.5 %all-gather = bf16[16,4,2048]{2,1,0:T(4,128)(2,1)S(1)} all-gather(bf16[1,4,2048]{2,1,0:T(4,128)(2,1)S(1)} %reshape.76), channel_id=1, replica_groups=mesh['grp'=2,'row'=8,'col'=2] {'row','col'}, dimensions={0}, use_global_device_ids=true | all-gather | bytes 278528 | tf_op jit(solution)/shard_map/all_gather | solution.py:282
  68.1 0.4 reshape.48.node_skel
  68.5 0.0 collective-permute-done.4
  68.6 0.0 collective-permute-done.5
  68.6 1.0 pad_maximum_fusion.skel
  69.6 0.0 copy-start.2
  69.6 0.0 collective-permute-done.2
  69.6 0.0 collective-permute-done.3
  69.7 1.0 copy-done.2
  70.6 97.7 %field.1 = bf16[32,32,128]{2,1,0:T(8,128)(2,1)} custom-call(s32[32,16]{1,0:T(8,128)S(1)} %compare_select_fusion.1.near_idx, s32[32]{0:T(128)S(1)} %get-tuple-element.25.near_cnt, s32[32,16]{1,0:T(8,128)S(1)} %compare_select_fusion.far_idx, s32[32]{0:T(128)S(1)} %get-tuple-element.11.far_cnt, s32[4,32]{1,0:T(4,128)S(1)} %compare_select_fusion.2.node_idx, ...), custom_call_target="tpu_custom_call" | custom-call | tf_op jit(solution)/shard_map/field/pallas_call | solution.py:217
  (28 shorter events, 0.3 us)
Async XLA Ops:
  0.0 36.0 %copy-start = (bf16[32,64,128]{2,1,0:T(8,128)(2,1)S(1)}, bf16[32,64,128]{2,1,0:T(8,128)(2,1)}, u32[]{:S(2)}) copy-start(bf16[32,64,128]{2,1,0:T(8,128)(2,1)} %param.16) | copy-start | bytes 1572868
  0.0 11.1 %copy-start.3 = (f32[6,4096]{1,0:T(8,128)S(1)}, f32[6,4096]{1,0:T(8,128)}, u32[]{:S(2)}) copy-start(f32[6,4096]{1,0:T(8,128)} %param.12) | copy-start | bytes 294916
  0.0 16.6 %copy-start.7 = (s32[32,16]{0,1:T(8,128)S(1)}, s32[32,16]{0,1:T(8,128)}, u32[]{:S(2)}) copy-start(s32[32,16]{0,1:T(8,128)} %param.13) | copy-start | bytes 6148
  0.0 16.7 %copy-start.6 = (s32[32,16]{0,1:T(8,128)S(1)}, s32[32,16]{0,1:T(8,128)}, u32[]{:S(2)}) copy-start(s32[32,16]{0,1:T(8,128)} %param.14) | copy-start | bytes 6148
  0.0 17.1 %copy-start.4 = (bf16[32,32,128]{2,1,0:T(8,128)(2,1)S(1)}, bf16[32,32,128]{2,1,0:T(8,128)(2,1)}, u32[]{:S(2)}) copy-start(bf16[32,32,128]{2,1,0:T(8,128)(2,1)} %param.10) | copy-start | bytes 786436
  3.8 15.9 %all-to-all-start.1 = ((s32[16,2,1]{1,2,0:T(1,128)}), s32[16,2,1]{1,2,0:T(1,128)S(1)}, u32[]{:S(2)}, u32[]{:S(2)}) async-start(s32[16,2,1]{1,2,0:T(1,128)} %bitcast.1), calls=%async_computation.1 | async-start | bytes 16384 | tf_op jit(solution)/shard_map/all_to_all | solution.py:262
  11.1 17.8 %collective-permute-start = (f32[8,2048]{1,0:T(8,128)S(1)}, f32[8,2048]{1,0:T(8,128)S(1)}, u32[]{:S(2)}, u32[]{:S(2)}) collective-permute-start(f32[8,2048]{1,0:T(8,128)S(1)} %get-tuple-element.19), channel_id=1, source_target_pairs={{0,1},{1,2},{2,3},{3,4},{4,5},{5,6},{6,7},{7,8},{8,9},{9,10},{10,1... | collective-permute-start | bytes 196616 | tf_op jit(solution)/shard_map/ppermute | solution.py:25
  14.7 14.3 %collective-permute-start.1 = (f32[8,2048]{1,0:T(8,128)S(1)}, f32[8,2048]{1,0:T(8,128)S(1)}, u32[]{:S(2)}, u32[]{:S(2)}) collective-permute-start(f32[8,2048]{1,0:T(8,128)S(1)} %get-tuple-element.20), channel_id=1, source_target_pairs={{1,0},{2,1},{3,2},{4,3},{5,4},{6,5},{7,6},{8,7},{9,8},{10,9},{11,1... | collective-permute-start | bytes 196616 | tf_op jit(solution)/shard_map/ppermute | solution.py:27
  16.7 2.4 %copy-start.8 = (s32[4,32]{1,0:T(4,128)S(1)}, s32[4,32]{1,0:T(4,128)}, u32[]{:S(2)}) copy-start(s32[4,32]{1,0:T(4,128)} %param.15) | copy-start | bytes 1540
  17.1 2.6 %copy-start.5 = (f32[3,4096]{1,0:T(4,128)S(1)}, f32[3,4096]{1,0:T(4,128)}, u32[]{:S(2)}) copy-start(f32[3,4096]{1,0:T(4,128)} %param.19) | copy-start | bytes 147460
  19.7 15.6 %all-to-all-start = ((bf16[32,32,128]{2,1,0:T(8,128)(2,1)}), bf16[32,32,128]{2,1,0:T(8,128)(2,1)S(1)}, u32[]{:S(2)}, u32[]{:S(2)}) async-start(bf16[32,32,128]{2,1,0:T(8,128)(2,1)} %gather_fusion), calls=%async_computation | async-start | bytes 524288 | tf_op jit(solution)/shard_map/all_to_all | solution.py:261
  36.4 9.9 %copy-start.1 = (bf16[4,64,512]{2,1,0:T(8,128)(2,1)S(1)}, bf16[4,64,512]{2,1,0:T(8,128)(2,1)}, u32[]{:S(2)}) copy-start(bf16[4,64,512]{2,1,0:T(8,128)(2,1)} %transfer.1) | copy-start | bytes 786436
  36.5 32.1 %collective-permute-start.4 = (bf16[16,32,64]{2,1,0:T(8,128)(2,1)S(1)}, bf16[16,32,64]{2,1,0:T(8,128)(2,1)S(1)}, u32[]{:S(2)}, u32[]{:S(2)}) collective-permute-start(bf16[16,32,64]{2,1,0:T(8,128)(2,1)S(1)} %get-tuple-element.15), channel_id=1, source_target_pairs={{0,1},{1,2},{2,3},{3,4},{4,5},{5,6},{6,7},{7,8},{8,9},{9,10},{10,1... | collective-permute-start | bytes 196616 | tf_op jit(solution)/shard_map/ppermute | solution.py:25
  38.5 30.0 %collective-permute-start.5 = (bf16[16,32,64]{2,1,0:T(8,128)(2,1)S(1)}, bf16[16,32,64]{2,1,0:T(8,128)(2,1)}, u32[]{:S(2)}, u32[]{:S(2)}) collective-permute-start(bf16[16,32,64]{2,1,0:T(8,128)(2,1)S(1)} %get-tuple-element.16), channel_id=1, source_target_pairs={{1,0},{2,1},{3,2},{4,3},{5,4},{6,5},{7,6},{8,7},{9,8},{10,9},{11,1... | collective-permute-start | bytes 196616 | tf_op jit(solution)/shard_map/ppermute | solution.py:27
  40.9 28.7 %collective-permute-start.2 = (bf16[16,32,128]{2,1,0:T(8,128)(2,1)S(1)}, bf16[16,32,128]{2,1,0:T(8,128)(2,1)S(1)}, u32[]{:S(2)}, u32[]{:S(2)}) collective-permute-start(bf16[16,32,128]{2,1,0:T(8,128)(2,1)S(1)} %get-tuple-element.17), channel_id=1, source_target_pairs={{0,1},{1,2},{2,3},{3,4},{4,5},{5,6},{6,7},{7,8},{8,9},{9,10},{10,1... | collective-permute-start | bytes 393224 | tf_op jit(solution)/shard_map/ppermute | solution.py:25
  44.1 25.5 %collective-permute-start.3 = (bf16[16,32,128]{2,1,0:T(8,128)(2,1)S(1)}, bf16[16,32,128]{2,1,0:T(8,128)(2,1)S(1)}, u32[]{:S(2)}, u32[]{:S(2)}) collective-permute-start(bf16[16,32,128]{2,1,0:T(8,128)(2,1)S(1)} %get-tuple-element.18), channel_id=1, source_target_pairs={{1,0},{2,1},{3,2},{4,3},{5,4},{6,5},{7,6},{8,7},{9,8},{10,9},{11,1... | collective-permute-start | bytes 393224 | tf_op jit(solution)/shard_map/ppermute | solution.py:27
  69.6 1.0 copy-start.2

commit v2 on v1

--- a/solution.py
+++ b/solution.py
@@ -77,15 +77,22 @@
     return xyz, target, source
 
 
-def halves(a, lane):
-    return jnp.where(lane < 64, a, 0.0), jnp.where(lane < 64, 0.0, pltpu.roll(a, 64, 1))
+def flat(count, chunk, size):
+    rows = count.shape[0]
+    chunks = (count + chunk - 1) // chunk
+    row_ids = jnp.arange(rows, dtype=jnp.int32)
+    end = jnp.sum(jnp.where(row_ids[:, None] >= row_ids, chunks, 0), axis=1)
+    g = jnp.arange(size, dtype=jnp.int32)
+    row = jnp.sum((end <= g[:, None]).astype(jnp.int32), axis=1)
+    start = jnp.sum(jnp.where(row_ids == row[:, None], end - chunks, 0), axis=1)
+    return row, jnp.where(row < rows, (g - start) * chunk, 0), jnp.sum(chunks).reshape(1)
 
 
 def field_kernel(
     wide, nodes, chunk,
-    near_idx, near_cnt, far_idx, far_cnt, node_idx, node_cnt, first_node,
+    near_idx, near_row, near_col, near_total, far_idx, far_row, far_col, far_total, first_node,
     geo, dens, skel, node_pts, node_skel, transfer, basis_out, out,
-    target_form, source_form, far_form, far_skel, node_target, node_form, node_dens, down,
+    target_form, source_form, far_target, far_form, far_skel, near_acc, far_acc, both, near_k, square, far_k,
 ):
     leaves, nrhs, leaf_size = out.shape
     nodes_here, rank, width = transfer.shape
@@ -94,46 +101,52 @@
     row = lax.broadcasted_iota(jnp.int32, (8, leaf_size), 0)
     lane = lax.broadcasted_iota(jnp.int32, (1, leaf_size), 1)
     low = lane < rank
+    base = wide + 1
+    group = 4
 
     def columns(ref, block):
         return ref[:, pl.ds(pl.multiple_of(block * leaf_size, leaf_size), leaf_size)]
 
-    def node_block(b, carry):
+    def each(count, body):
+        def step(i, carry):
+            for k in range(group):
+                body(i * group + k)
+            return carry
+
+        lax.fori_loop(0, count // group, step, 0)
+
+    def node_block(b):
         _, _, source = point_forms(columns(node_pts, b), row)
         form = right_side(source)
         turned = pltpu.roll(form, rank, 1)
-        node_form[0, 2 * b] = jnp.where(low, form, 0.0).astype(bf16)
-        node_form[1, 2 * b] = jnp.where(low, 0.0, turned).astype(bf16)
-        node_form[0, 2 * b + 1] = jnp.where(low, turned, 0.0).astype(bf16)
-        node_form[1, 2 * b + 1] = jnp.where(low, 0.0, form).astype(bf16)
-        return carry
-
-    lax.fori_loop(0, nodes // 2, node_block, 0)
-    node_form[0, nodes] = node_form[0, 0]
-    node_form[1, nodes] = node_form[1, 0]
-
-    def spread(skel_ref, spread_ref, count):
-        def step(s, carry):
-            both = jnp.concatenate([skel_ref[s], skel_ref[s]], axis=1)
-            none = jnp.zeros_like(both)
-            spread_ref[0, s] = jnp.where(low, both, none)
-            spread_ref[1, s] = jnp.where(low, none, both)
-            return carry
-
-        lax.fori_loop(0, count, step, 0)
-        spread_ref[0, count] = jnp.zeros((nrhs, leaf_size), bf16)
-        spread_ref[1, count] = jnp.zeros((nrhs, leaf_size), bf16)
-
-    spread(node_skel, node_dens, nodes)
-    spread(skel, far_skel, wide)
+        far_form[0, base + 2 * b] = jnp.where(low, form, 0.0).astype(bf16)
+        far_form[1, base + 2 * b] = jnp.where(low, 0.0, turned).astype(bf16)
+        far_form[0, base + 2 * b + 1] = jnp.where(low, turned, 0.0).astype(bf16)
+        far_form[1, base + 2 * b + 1] = jnp.where(low, 0.0, form).astype(bf16)
+
+    each(nodes // 2, node_block)
+
+    def spread(skel_ref, first):
+        def step(s):
+            both_halves = jnp.concatenate([skel_ref[s], skel_ref[s]], axis=1)
+            none = jnp.zeros_like(both_halves)
+            far_skel[0, first + s] = jnp.where(low, both_halves, none)
+            far_skel[1, first + s] = jnp.where(low, none, both_halves)
+
+        each(skel_ref.shape[0], step)
+
+    spread(node_skel, base)
+    spread(skel, 0)
+    far_skel[0, wide] = jnp.zeros((nrhs, leaf_size), bf16)
+    far_skel[1, wide] = jnp.zeros((nrhs, leaf_size), bf16)
 
     for b in range(nodes_here // 2):
         _, target, _ = point_forms(columns(node_pts, first_node[0] // 2 + b), row)
         turned = left_side(target).T.astype(bf16)
-        node_target[2 * b] = turned[:rank]
-        node_target[2 * b + 1] = turned[rank:]
-
-    def leaf_block(s, carry):
+        far_target[leaves + 2 * b] = turned[:rank]
+        far_target[leaves + 2 * b + 1] = turned[rank:]
+
+    def leaf_block(s):
         points = columns(geo, s)
         xyz, target, source = point_forms(points, row)
         normal = jnp.where(row < 3, pltpu.roll(points, 5, 0), 0.0) * inv_four_pi
@@ -143,66 +156,86 @@
         source_form[s] = jnp.concatenate([form, right_side(normal)], axis=1).astype(bf16)
         far_form[0, s] = jnp.where(low, form, 0.0).astype(bf16)
         far_form[1, s] = jnp.where(low, 0.0, pltpu.roll(form, rank, 1)).astype(bf16)
-        return carry
-
-    lax.fori_loop(0, wide, leaf_block, 0)
+
+    each(wide, leaf_block)
     source_form[wide] = source_form[0]
     far_form[0, wide] = far_form[0, 0]
     far_form[1, wide] = far_form[1, 0]
 
-    def own_block(t, carry):
+    def own_block(t):
         _, target, _ = point_forms(columns(geo, t + REACH), row)
-        target_form[t] = left_side(target).T.astype(bf16)
-        return carry
-
-    lax.fori_loop(0, leaves, own_block, 0)
-
-    def coupled(idx, count, t, form, points, charges):
-        def step(c, acc):
-            ids = [idx[t, c * chunk + k] for k in range(chunk)]
-            weights = jnp.concatenate(
-                [points[0, ids[k]] + points[1, ids[k + 1]] for k in range(0, chunk, 2)], axis=1
-            )
-            square = jnp.dot(form, weights, preferred_element_type=f32)
-            kernel = (inv_four_pi * lax.rsqrt(square)).astype(bf16)
-            charge = jnp.concatenate(
-                [charges[0, ids[k]] + charges[1, ids[k + 1]] for k in range(0, chunk, 2)], axis=1
-            )
-            return acc + lax.dot_general(charge, kernel, NT, preferred_element_type=f32)
-
-        return lax.fori_loop(0, (count[t] + chunk - 1) // chunk, step, jnp.zeros((nrhs, rank), f32))
-
+        turned = left_side(target).T.astype(bf16)
+        target_form[t] = turned
+        far_target[t] = turned[:rank]
+        near_acc[t] = jnp.zeros((nrhs, leaf_size), f32)
+        far_acc[t] = jnp.zeros((nrhs, rank), f32)
+
+    each(leaves, own_block)
     for p in range(nodes_here):
-        far = coupled(node_idx, node_cnt, p, node_target[p], node_form, node_dens).astype(bf16)
+        far_acc[leaves + p] = jnp.zeros((nrhs, rank), f32)
+
+    def pipeline(idx, rows_of, cols_of, total, rows, first, middle, last):
+        def ids_of(g):
+            t, c = jnp.minimum(rows_of[g], rows - 1), cols_of[g]
+            return t, [idx[t, c + k] for k in range(chunk)]
+
+        def step(g, carry):
+            old = jnp.maximum(g - 2, 0)
+            last(jnp.where(g >= 2, rows_of[old], rows), ids_of(old)[1])
+            middle()
+            first(*ids_of(g))
+            return carry
+
+        lax.fori_loop(0, total[0] + 2, step, 0)
+
+    def far_first(t, ids):
+        weights = jnp.concatenate(
+            [far_form[0, ids[k]] + far_form[1, ids[k + 1]] for k in range(0, chunk, 2)], axis=1
+        )
+        square[...] = jnp.dot(far_target[t], weights, preferred_element_type=f32)
+
+    def far_middle():
+        far_k[...] = (inv_four_pi * lax.rsqrt(square[...])).astype(bf16)
+
+    def far_last(t, ids):
+        charge = jnp.concatenate(
+            [far_skel[0, ids[k]] + far_skel[1, ids[k + 1]] for k in range(0, chunk, 2)], axis=1
+        )
+        far_acc[t] += lax.dot_general(charge, far_k[...], NT, preferred_element_type=f32)
+
+    pipeline(
+        far_idx, far_row, far_col, far_total, leaves + nodes_here, far_first, far_middle, far_last
+    )
+
+    def near_first(t, ids):
+        form = target_form[t]
+        for k in range(chunk):
+            both[k] = jnp.dot(form, source_form[ids[k]], preferred_element_type=f32)
+
+    def near_middle():
+        for k in range(chunk):
+            r = lax.rsqrt(both[k, :, :leaf_size])
+            near_k[:, k * leaf_size : (k + 1) * leaf_size] = (
+                both[k, :, leaf_size:] * (r * r * r)
+            ).astype(bf16)
+
+    def near_last(t, ids):
+        charge = jnp.concatenate([dens[ids[k]] for k in range(chunk)], axis=1)
+        near_acc[t] += lax.dot_general(charge, near_k[...], NT, preferred_element_type=f32)
+
+    pipeline(
+        near_idx, near_row, near_col, near_total, leaves, near_first, near_middle, near_last
+    )
+
+    for p in range(nodes_here):
+        far = far_acc[leaves + p].astype(bf16)
         spreading = jnp.dot(far, transfer[p], preferred_element_type=f32)
         for c in range(children):
-            down[p * children + c] = spreading[:, c * rank : (c + 1) * rank]
-
-    def leaf(t, carry):
-        form = target_form[t]
-        far = coupled(far_idx, far_cnt, t, form[:rank], far_form, far_skel)
-        local = (far + down[t]).astype(bf16)
-        start = jnp.dot(local, basis_out[t], preferred_element_type=f32)
-
-        def step(c, acc):
-            kernels, charges = [], []
-            for k in range(chunk):
-                s = near_idx[t, c * chunk + k]
-                both = jnp.dot(form, source_form[s], preferred_element_type=f32)
-                r = lax.rsqrt(both[:, :leaf_size])
-                kernels.append((both[:, leaf_size:] * (r * r * r)).astype(bf16))
-                charges.append(dens[s])
-            return acc + lax.dot_general(
-                jnp.concatenate(charges, axis=1),
-                jnp.concatenate(kernels, axis=1),
-                NT,
-                preferred_element_type=f32,
-            )
-
-        out[t] = lax.fori_loop(0, (near_cnt[t] + chunk - 1) // chunk, step, start).astype(bf16)
-        return carry
-
-    lax.fori_loop(0, leaves, leaf, 0)
+            t = p * children + c
+            local = (far_acc[t] + spreading[:, c * rank : (c + 1) * rank]).astype(bf16)
+            out[t] = (
+                near_acc[t] + jnp.dot(local, basis_out[t], preferred_element_type=f32)
+            ).astype(bf16)
 
 
 def field(near, far, node, first_node, geo, dens, skel, node_pts, node_skel, transfer, basis_out):
@@ -210,28 +243,48 @@
     nrhs, leaf_size = dens.shape[1:]
     nodes_here, rank, width = transfer.shape
     leaves = basis_out.shape[0]
-    terms = 48
-    bf16 = jnp.bfloat16
+    terms, chunk = 48, 4
+    bf16, f32 = jnp.bfloat16, jnp.float32
+    near_idx, near_count = near
+    far_idx, far_count = far
+    node_idx, node_count = node
+    slots = node_idx.shape[1]
+    far_size = (far_idx.size + node_idx.size) // chunk + 2
+    far_idx = jnp.concatenate(
+        [
+            jnp.pad(far_idx, ((0, 0), (0, slots - far_idx.shape[1])), constant_values=wide),
+            node_idx,
+        ],
+        axis=0,
+    )
+    far_count = jnp.concatenate([far_count, node_count])
     smem = pl.BlockSpec(memory_space=pltpu.SMEM)
     vmem = pl.BlockSpec(memory_space=pltpu.VMEM)
     return pl.pallas_call(
-        functools.partial(field_kernel, wide, nodes, 4),
+        functools.partial(field_kernel, wide, nodes, chunk),
         out_shape=jax.ShapeDtypeStruct((leaves, nrhs, leaf_size), bf16),
-        in_specs=[smem] * 7 + [vmem] * 7,
+        in_specs=[smem] * 9 + [vmem] * 7,
         out_specs=vmem,
         scratch_shapes=[
             pltpu.VMEM((leaves, leaf_size, terms), bf16),
             pltpu.VMEM((wide + 1, terms, 2 * leaf_size), bf16),
-            pltpu.VMEM((2, wide + 1, terms, leaf_size), bf16),
-            pltpu.VMEM((2, wide + 1, nrhs, leaf_size), bf16),
-            pltpu.VMEM((nodes_here, rank, terms), bf16),
-            pltpu.VMEM((2, nodes + 1, terms, leaf_size), bf16),
-            pltpu.VMEM((2, nodes + 1, nrhs, leaf_size), bf16),
-            pltpu.VMEM((leaves, nrhs, rank), jnp.float32),
+            pltpu.VMEM((leaves + nodes_here, rank, terms), bf16),
+            pltpu.VMEM((2, wide + 1 + nodes, terms, leaf_size), bf16),
+            pltpu.VMEM((2, wide + 1 + nodes, nrhs, leaf_size), bf16),
+            pltpu.VMEM((leaves + 1, nrhs, leaf_size), f32),
+            pltpu.VMEM((leaves + nodes_here + 1, nrhs, rank), f32),
+            pltpu.VMEM((chunk, leaf_size, 2 * leaf_size), f32),
+            pltpu.VMEM((leaf_size, chunk * leaf_size), bf16),
+            pltpu.VMEM((rank, chunk * rank), f32),
+            pltpu.VMEM((rank, chunk * rank), bf16),
         ],
         compiler_params=pltpu.CompilerParams(vmem_limit_bytes=48 * 1024 * 1024),
         name="field",
-    )(*near, *far, *node, first_node, geo, dens, skel, node_pts, node_skel, transfer, basis_out)
+    )(
+        near_idx, *flat(near_count, chunk, near_idx.size // chunk + 2),
+        far_idx, *flat(far_count, chunk, far_size),
+        first_node, geo, dens, skel, node_pts, node_skel, transfer, basis_out,
+    )
 
 
 def on_device(
@@ -282,10 +335,9 @@
     all_skel = lax.all_gather(
         node_skel.reshape(nodes_here, nrhs_here * rank_size), ("row", "col"), axis=0, tiled=True
     ).reshape(-1, nrhs_here, rank_size)
-    nodes = all_skel.shape[0]
     near = fill(compacted(near_list, REACH - first_leaf, wide))
     far = fill(compacted(far_list, REACH - first_leaf, wide))
-    node = fill(compacted(node_list, 0, nodes))
+    node = fill(compacted(node_list, wide + 1, wide))
     first_node = (first_leaf // children).reshape(1)
     node_pts = jnp.pad(node_points, ((0, 5), (0, 0)))
     return field(

time: 171 us -> 129 us (0.75)
  Pallas kernels: 97.7 us -> 54.3 us
  other arithmetic: 6.9 us -> 9.07 us
    pallas_call x1, Pallas kernels: 97.7 us -> 54.3 us  [field(): pl.pallas_call(functools.partial(field_kernel, wide, nodes, chunk), out_s...]
    reduce_sum x0 -> x8, other arithmetic: none -> 2.02 us  [the longest x2 1.43 us: flat(): jnp.sum(chunks).reshape(1)]
  transfers between devices with their start and end apart: 8 -> 8, of which waited for: 1 -> 1; matrix products, arithmetic and copies ran while one was open for 5% -> 8% of each run, Pallas kernels for 0% -> 0%
where the time goes in v2:
time: 129 us; the launch traced here: 127 us
  Pallas kernels  54.3 us (42%)
  starting transfers between devices  28.5 us (22%)
  blocking collectives  21.5 us (17%)
  other arithmetic  9.07 us (7%)
  local copies, waits for them, and re-layouts  6.52 us (5%)
  waiting for transfers between devices  6.38 us (5%)
    pallas_call x1, Pallas kernels, field(): pl.pallas_call(functools.partial(field_kernel, wide, nodes, chunk), out_s...  54.3 us
    all_gather x1, blocking collectives, on_device(): lax.all_gather(node_skel.reshape(nodes_here, nrhs_here * rank_size), ('ro...  21.5 us
    ppermute x3, starting transfers between devices, extended(): lax.ppermute(tail, axis, [(i, (i + 1) % count) for i in range(ends)])  8.75 us
    all_to_all x1, starting transfers between devices, on_device(): lax.all_to_all(out_slot, ('row', 'col'), split_axis=0, concat_axis=0, til...  7.34 us
    all_to_all x1, waiting for transfers between devices, on_device(): lax.all_to_all(outgoing, ('row', 'col'), split_axis=0, concat_axis=0, til...  6.36 us
    ppermute x3, starting transfers between devices, extended(): lax.ppermute(head, axis, [((i + 1) % count, i) for i in range(ends)])  6.25 us
    all_to_all x1, starting transfers between devices, on_device(): lax.all_to_all(outgoing, ('row', 'col'), split_axis=0, concat_axis=0, til...  6.13 us
  transfers between devices with their start and end apart: 8, of which 1 were waited for; matrix products, arithmetic and copies ran while one was open for 8% of the time, Pallas kernels for 0%

profile of v2, /device:TPU:1, one launch (start us, length us, event | category | flops | bytes accessed | tf_op | source)
XLA Modules:
  0.0 127.2 jit_solution(5470205408403251828)
XLA Ops:
  0.0 0.0 copy-start
  0.0 0.7 and_select_fusion
  0.8 1.6 %sort.34 = (s32[32]{0:T(128)}, s32[32]{0:T(128)S(1)}) sort(s32[32]{0:T(128)S(1)} %get-tuple-element.27, s32[32]{0:T(128)S(1)} %iota.47), dimensions={0}, to_apply=%region_17.18 | sort | flops 160 | bytes 512 | tf_op jit(solution)/shard_map/jit(argsort)/sort | solution.py:310
  2.4 0.7 gather_fusion.1
  3.1 0.7 all_to_all.12
  3.8 7.3 %all-to-all-start.1 = ((s32[16,2,1]{1,2,0:T(1,128)}), s32[16,2,1]{1,2,0:T(1,128)S(1)}, u32[]{:S(2)}, u32[]{:S(2)}) async-start(s32[16,2,1]{1,2,0:T(1,128)} %bitcast.3), calls=%async_computation.1 | async-start | bytes 16384 | tf_op jit(solution)/shard_map/all_to_all | solution.py:315
  11.1 0.0 copy-done.3
  11.2 3.5 %collective-permute-start = (f32[8,2048]{1,0:T(8,128)S(1)}, f32[8,2048]{1,0:T(8,128)S(1)}, u32[]{:S(2)}, u32[]{:S(2)}) collective-permute-start(f32[8,2048]{1,0:T(8,128)S(1)} %get-tuple-element.23), channel_id=1, source_target_pairs={{0,1},{1,2},{2,3},{3,4},{4,5},{5,6},{6,7},{7,8},{8,9},{9,10},{10,1... | collective-permute-start | bytes 196616 | tf_op jit(solution)/shard_map/ppermute | solution.py:25
  14.7 1.9 %collective-permute-start.1 = (f32[8,2048]{1,0:T(8,128)S(1)}, f32[8,2048]{1,0:T(8,128)S(1)}, u32[]{:S(2)}, u32[]{:S(2)}) collective-permute-start(f32[8,2048]{1,0:T(8,128)S(1)} %get-tuple-element.24), channel_id=1, source_target_pairs={{1,0},{2,1},{3,2},{4,3},{5,4},{6,5},{7,6},{8,7},{9,8},{10,9},{11,1... | collective-permute-start | bytes 196616 | tf_op jit(solution)/shard_map/ppermute | solution.py:27
  16.7 0.1 convert_reduce_fusion.4
  16.8 0.1 copy.32
  16.8 0.1 convert_reduce_fusion.2
  17.0 0.8 fusion.8
  17.8 0.1 select_reduce_fusion.5
  17.9 0.1 convert_reduce_fusion.far_row
  18.0 0.1 copy.33
  18.1 0.1 copy.27
  18.1 0.1 convert_reduce_fusion.3
  18.3 0.6 fusion.9
  18.9 0.1 select_reduce_fusion.6
  19.0 0.1 convert_reduce_fusion.1.near_row
  19.1 0.1 copy.28
  19.2 1.3 %gather_fusion = bf16[32,32,128]{2,1,0:T(8,128)(2,1)} fusion(bf16[32,32,128]{2,1,0:T(8,128)(2,1)S(1)} %copy-done.4, s32[1024]{0:T(1024)S(1)} %pad_clamp_fusion.1), kind=kCustom, calls=%fused_computation | custom fusion | bytes 524416 | tf_op jit(solution)/shard_map/gather | solution.py:311
  20.5 0.1 select_reduce_fusion.3
  20.6 0.2 reduce_window_sum.29
  20.8 0.1 copy.34
  20.9 0.1 copy.35
  21.0 0.2 reduce_window_sum.30
  21.2 0.1 select_reduce_fusion.2
  21.4 0.1 select_reduce_fusion.4
  21.5 0.2 reduce_window_sum.28
  21.7 0.1 copy.29
  21.8 0.1 copy.30
  21.9 0.0 copy-done.5
  21.9 0.0 all-to-all-done.1
  22.0 6.1 %all-to-all-start = ((bf16[32,32,128]{2,1,0:T(8,128)(2,1)}), bf16[32,32,128]{2,1,0:T(8,128)(2,1)S(1)}, u32[]{:S(2)}, u32[]{:S(2)}) async-start(bf16[32,32,128]{2,1,0:T(8,128)(2,1)} %gather_fusion), calls=%async_computation | async-start | bytes 524288 | tf_op jit(solution)/shard_map/all_to_all | solution.py:314
  28.1 0.6 broadcast.139
  28.7 0.7 reduce.3
  29.4 0.1 all_to_all.14
  29.5 1.7 %sort.35 = (s32[32]{0:T(128)}, s32[32]{0:T(128)S(1)}) sort(s32[32]{0:T(128)S(1)} %all_to_all.14, s32[32]{0:T(128)S(1)} %iota.48), dimensions={0}, to_apply=%region_18.19 | sort | flops 160 | bytes 512 | tf_op jit(solution)/shard_map/jit(argsort)/sort | solution.py:317
  31.2 0.0 collective-permute-done
  31.2 0.0 collective-permute-done.1
  31.2 6.4 %all-to-all-done = bf16[32,32,128]{2,1,0:T(8,128)(2,1)S(1)} async-done(((bf16[32,32,128]{2,1,0:T(8,128)(2,1)}), bf16[32,32,128]{2,1,0:T(8,128)(2,1)S(1)}, u32[]{:S(2)}, u32[]{:S(2)}) %all-to-all-start) | async-done | bytes 262176 | tf_op jit(solution)/shard_map/all_to_all | solution.py:314
  37.6 0.6 gather_fusion.2
  38.2 0.4 convolution_convert_fusion
  38.7 0.0 copy-start.1
  38.7 2.1 %collective-permute-start.4 = (bf16[16,32,64]{2,1,0:T(8,128)(2,1)S(1)}, bf16[16,32,64]{2,1,0:T(8,128)(2,1)S(1)}, u32[]{:S(2)}, u32[]{:S(2)}) collective-permute-start(bf16[16,32,64]{2,1,0:T(8,128)(2,1)S(1)} %get-tuple-element.19), channel_id=1, source_target_pairs={{0,1},{1,2},{2,3},{3,4},{4,5},{5,6},{6,7},{7,8},{8,9},{9,10},{10,1... | collective-permute-start | bytes 196616 | tf_op jit(solution)/shard_map/ppermute | solution.py:25
  40.7 2.4 %collective-permute-start.5 = (bf16[16,32,64]{2,1,0:T(8,128)(2,1)S(1)}, bf16[16,32,64]{2,1,0:T(8,128)(2,1)}, u32[]{:S(2)}, u32[]{:S(2)}) collective-permute-start(bf16[16,32,64]{2,1,0:T(8,128)(2,1)S(1)} %get-tuple-element.20), channel_id=1, source_target_pairs={{1,0},{2,1},{3,2},{4,3},{5,4},{6,5},{7,6},{8,7},{9,8},{10,9},{11,1... | collective-permute-start | bytes 196616 | tf_op jit(solution)/shard_map/ppermute | solution.py:27
  43.2 3.2 %collective-permute-start.2 = (bf16[16,32,128]{2,1,0:T(8,128)(2,1)S(1)}, bf16[16,32,128]{2,1,0:T(8,128)(2,1)S(1)}, u32[]{:S(2)}, u32[]{:S(2)}) collective-permute-start(bf16[16,32,128]{2,1,0:T(8,128)(2,1)S(1)} %get-tuple-element.21), channel_id=1, source_target_pairs={{0,1},{1,2},{2,3},{3,4},{4,5},{5,6},{6,7},{7,8},{8,9},{9,10},{10,1... | collective-permute-start | bytes 393224 | tf_op jit(solution)/shard_map/ppermute | solution.py:25
  46.3 1.9 %collective-permute-start.3 = (bf16[16,32,128]{2,1,0:T(8,128)(2,1)S(1)}, bf16[16,32,128]{2,1,0:T(8,128)(2,1)S(1)}, u32[]{:S(2)}, u32[]{:S(2)}) collective-permute-start(bf16[16,32,128]{2,1,0:T(8,128)(2,1)S(1)} %get-tuple-element.22), channel_id=1, source_target_pairs={{1,0},{2,1},{3,2},{4,3},{5,4},{6,5},{7,6},{8,7},{9,8},{10,9},{11,1... | collective-permute-start | bytes 393224 | tf_op jit(solution)/shard_map/ppermute | solution.py:27
  48.3 0.1 copy.38
  48.4 0.2 reshape.58
  48.6 0.2 convolution_convert_fusion.1
  48.8 0.1 reshape.88
  48.9 21.5 %all-gather = bf16[16,4,2048]{2,1,0:T(4,128)(2,1)S(1)} all-gather(bf16[1,4,2048]{2,1,0:T(4,128)(2,1)S(1)} %reshape.88), channel_id=1, replica_groups=mesh['grp'=2,'row'=8,'col'=2] {'row','col'}, dimensions={0}, use_global_device_ids=true | all-gather | bytes 278528 | tf_op jit(solution)/shard_map/all_gather | solution.py:335
  70.3 0.4 reshape.60.node_skel
  70.8 0.0 collective-permute-done.4
  70.8 0.0 collective-permute-done.5
  70.8 1.0 pad_maximum_fusion.skel
  71.8 0.0 copy-start.2
  71.8 0.0 collective-permute-done.2
  71.9 0.0 collective-permute-done.3
  71.9 1.0 copy-done.2
  72.9 54.3 %field.1 = bf16[32,32,128]{2,1,0:T(8,128)(2,1)} custom-call(s32[32,16]{1,0:T(8,128)S(1)} %compare_select_fusion.1.near_idx, s32[130]{0:T(256)S(1)} %convert_reduce_fusion.1.near_row, s32[130]{0:T(256)S(1)} %compare_select_fusion.6.near_col, s32[1]{0:T(128)} %bitcast.near_total, s32[36,32]{1,0:T(8,128)S(1)} %select_add_fusion.far_idx, ...), custom_call_target="tpu_custom_call" | custom-call | tf_op jit(solution)/shard_map/field/pallas_call | solution.py:263
  (42 shorter events, 0.4 us)
Async XLA Ops:
  0.0 38.2 %copy-start = (bf16[32,64,128]{2,1,0:T(8,128)(2,1)S(1)}, bf16[32,64,128]{2,1,0:T(8,128)(2,1)}, u32[]{:S(2)}) copy-start(bf16[32,64,128]{2,1,0:T(8,128)(2,1)} %param.16) | copy-start | bytes 1572868
  0.0 11.1 %copy-start.3 = (f32[6,4096]{1,0:T(8,128)S(1)}, f32[6,4096]{1,0:T(8,128)}, u32[]{:S(2)}) copy-start(f32[6,4096]{1,0:T(8,128)} %param.12) | copy-start | bytes 294916
  0.0 16.6 %copy-start.8 = (s32[4,32]{1,0:T(4,128)S(1)}, s32[4,32]{1,0:T(4,128)}, u32[]{:S(2)}) copy-start(s32[4,32]{1,0:T(4,128)} %param.15) | copy-start | bytes 1540
  0.0 16.8 %copy-start.6 = (s32[32,16]{0,1:T(8,128)S(1)}, s32[32,16]{0,1:T(8,128)}, u32[]{:S(2)}) copy-start(s32[32,16]{0,1:T(8,128)} %param.14) | copy-start | bytes 6148
  0.0 18.0 %copy-start.7 = (s32[32,16]{0,1:T(8,128)S(1)}, s32[32,16]{0,1:T(8,128)}, u32[]{:S(2)}) copy-start(s32[32,16]{0,1:T(8,128)} %param.13) | copy-start | bytes 6148
  0.0 19.2 %copy-start.4 = (bf16[32,32,128]{2,1,0:T(8,128)(2,1)S(1)}, bf16[32,32,128]{2,1,0:T(8,128)(2,1)}, u32[]{:S(2)}) copy-start(bf16[32,32,128]{2,1,0:T(8,128)(2,1)} %param.10) | copy-start | bytes 786436
  3.8 18.2 %all-to-all-start.1 = ((s32[16,2,1]{1,2,0:T(1,128)}), s32[16,2,1]{1,2,0:T(1,128)S(1)}, u32[]{:S(2)}, u32[]{:S(2)}) async-start(s32[16,2,1]{1,2,0:T(1,128)} %bitcast.3), calls=%async_computation.1 | async-start | bytes 16384 | tf_op jit(solution)/shard_map/all_to_all | solution.py:315
  11.2 20.0 %collective-permute-start = (f32[8,2048]{1,0:T(8,128)S(1)}, f32[8,2048]{1,0:T(8,128)S(1)}, u32[]{:S(2)}, u32[]{:S(2)}) collective-permute-start(f32[8,2048]{1,0:T(8,128)S(1)} %get-tuple-element.23), channel_id=1, source_target_pairs={{0,1},{1,2},{2,3},{3,4},{4,5},{5,6},{6,7},{7,8},{8,9},{9,10},{10,1... | collective-permute-start | bytes 196616 | tf_op jit(solution)/shard_map/ppermute | solution.py:25
  14.7 16.5 %collective-permute-start.1 = (f32[8,2048]{1,0:T(8,128)S(1)}, f32[8,2048]{1,0:T(8,128)S(1)}, u32[]{:S(2)}, u32[]{:S(2)}) collective-permute-start(f32[8,2048]{1,0:T(8,128)S(1)} %get-tuple-element.24), channel_id=1, source_target_pairs={{1,0},{2,1},{3,2},{4,3},{5,4},{6,5},{7,6},{8,7},{9,8},{10,9},{11,1... | collective-permute-start | bytes 196616 | tf_op jit(solution)/shard_map/ppermute | solution.py:27
  19.2 2.7 %copy-start.5 = (f32[3,4096]{1,0:T(4,128)S(1)}, f32[3,4096]{1,0:T(4,128)}, u32[]{:S(2)}) copy-start(f32[3,4096]{1,0:T(4,128)} %param.19) | copy-start | bytes 147460
  22.0 15.6 %all-to-all-start = ((bf16[32,32,128]{2,1,0:T(8,128)(2,1)}), bf16[32,32,128]{2,1,0:T(8,128)(2,1)S(1)}, u32[]{:S(2)}, u32[]{:S(2)}) async-start(bf16[32,32,128]{2,1,0:T(8,128)(2,1)} %gather_fusion), calls=%async_computation | async-start | bytes 524288 | tf_op jit(solution)/shard_map/all_to_all | solution.py:314
  38.7 9.9 %copy-start.1 = (bf16[4,64,512]{2,1,0:T(8,128)(2,1)S(1)}, bf16[4,64,512]{2,1,0:T(8,128)(2,1)}, u32[]{:S(2)}) copy-start(bf16[4,64,512]{2,1,0:T(8,128)(2,1)} %transfer.1) | copy-start | bytes 786436
  38.7 32.1 %collective-permute-start.4 = (bf16[16,32,64]{2,1,0:T(8,128)(2,1)S(1)}, bf16[16,32,64]{2,1,0:T(8,128)(2,1)S(1)}, u32[]{:S(2)}, u32[]{:S(2)}) collective-permute-start(bf16[16,32,64]{2,1,0:T(8,128)(2,1)S(1)} %get-tuple-element.19), channel_id=1, source_target_pairs={{0,1},{1,2},{2,3},{3,4},{4,5},{5,6},{6,7},{7,8},{8,9},{9,10},{10,1... | collective-permute-start | bytes 196616 | tf_op jit(solution)/shard_map/ppermute | solution.py:25
  40.7 30.0 %collective-permute-start.5 = (bf16[16,32,64]{2,1,0:T(8,128)(2,1)S(1)}, bf16[16,32,64]{2,1,0:T(8,128)(2,1)}, u32[]{:S(2)}, u32[]{:S(2)}) collective-permute-start(bf16[16,32,64]{2,1,0:T(8,128)(2,1)S(1)} %get-tuple-element.20), channel_id=1, source_target_pairs={{1,0},{2,1},{3,2},{4,3},{5,4},{6,5},{7,6},{8,7},{9,8},{10,9},{11,1... | collective-permute-start | bytes 196616 | tf_op jit(solution)/shard_map/ppermute | solution.py:27
  43.2 28.7 %collective-permute-start.2 = (bf16[16,32,128]{2,1,0:T(8,128)(2,1)S(1)}, bf16[16,32,128]{2,1,0:T(8,128)(2,1)S(1)}, u32[]{:S(2)}, u32[]{:S(2)}) collective-permute-start(bf16[16,32,128]{2,1,0:T(8,128)(2,1)S(1)} %get-tuple-element.21), channel_id=1, source_target_pairs={{0,1},{1,2},{2,3},{3,4},{4,5},{5,6},{6,7},{7,8},{8,9},{9,10},{10,1... | collective-permute-start | bytes 393224 | tf_op jit(solution)/shard_map/ppermute | solution.py:25
  46.3 25.5 %collective-permute-start.3 = (bf16[16,32,128]{2,1,0:T(8,128)(2,1)S(1)}, bf16[16,32,128]{2,1,0:T(8,128)(2,1)S(1)}, u32[]{:S(2)}, u32[]{:S(2)}) collective-permute-start(bf16[16,32,128]{2,1,0:T(8,128)(2,1)S(1)} %get-tuple-element.22), channel_id=1, source_target_pairs={{1,0},{2,1},{3,2},{4,3},{5,4},{6,5},{7,6},{8,7},{9,8},{10,9},{11,1... | collective-permute-start | bytes 393224 | tf_op jit(solution)/shard_map/ppermute | solution.py:27
  71.8 1.0 copy-start.2

commit v3 on v2

--- a/solution.py
+++ b/solution.py
@@ -12,23 +12,6 @@
 smoothing = 0.1
 inv_four_pi = 0.25 / math.pi
 NT = (((1,), (1,)), ((), ()))
-
-
-def extended(cells, sides, width):
-    for axis, dim in sides:
-        count = lax.axis_size(axis)
-        ends = count - 1
-        head = lax.slice_in_dim(cells, 0, width, axis=dim)
-        tail = lax.slice_in_dim(cells, cells.shape[dim] - width, cells.shape[dim], axis=dim)
-        cells = jnp.concatenate(
-            [
-                lax.ppermute(tail, axis, [(i, (i + 1) % count) for i in range(ends)]),
-                cells,
-                lax.ppermute(head, axis, [((i + 1) % count, i) for i in range(ends)]),
-            ],
-            axis=dim,
-        )
-    return cells
 
 
 def compacted(entries, base, pad):
@@ -287,6 +270,99 @@
     )
 
 
+def peers():
+    columns = lax.axis_size("col")
+    count = lax.axis_size("row") * columns
+    me = lax.axis_index("row") * columns + lax.axis_index("col")
+
+    def peer(k):
+        q = lax.rem(me + k, count)
+        return q, {"row": q // columns, "col": lax.rem(q, columns)}
+
+    return me, count, peer
+
+
+def greet(count, peer):
+    barrier = pltpu.get_barrier_semaphore()
+    for k in range(1, count):
+        pl.semaphore_signal(
+            barrier, inc=1, device_id=peer(k)[1], device_id_type=pl.DeviceIdType.MESH
+        )
+    pl.semaphore_wait(barrier, count - 1)
+
+
+def sender(send_sem, recv_sem):
+    copies = []
+
+    def send(src, dst, where):
+        k = len(copies)
+        copy = pltpu.make_async_remote_copy(
+            src_ref=src,
+            dst_ref=dst,
+            send_sem=send_sem.at[k],
+            recv_sem=recv_sem.at[k],
+            device_id=where,
+            device_id_type=pl.DeviceIdType.MESH,
+        )
+        copy.start()
+        copies.append(copy)
+
+    return copies, send
+
+
+def exchange_kernel(outgoing, slots, geo, arrived, arrived_slots, geo_wide, send_sem, recv_sem):
+    me, count, peer = peers()
+    per = outgoing.shape[0] // count
+    inner = geo.shape[1]
+    halo = (geo_wide.shape[1] - inner) // 2
+    greet(count, peer)
+    copies, send = sender(send_sem, recv_sem)
+    for k in range(1, count):
+        q, where = peer(k)
+        send(slots.at[q], arrived_slots.at[me], where)
+        send(outgoing.at[pl.ds(q * per, per)], arrived.at[pl.ds(me * per, per)], where)
+    send(geo.at[:, pl.ds(inner - halo, halo)], geo_wide.at[:, pl.ds(0, halo)], peer(1)[1])
+    send(geo.at[:, pl.ds(0, halo)], geo_wide.at[:, pl.ds(halo + inner, halo)], peer(count - 1)[1])
+    arrived_slots[me] = slots[me]
+    for k in range(per):
+        arrived[me * per + k] = outgoing[me * per + k]
+    geo_wide[:, halo : halo + inner] = geo[...]
+    for copy in copies:
+        copy.wait()
+
+
+def share_kernel(dens, skel, node_skel, dens_wide, skel_wide, all_skel, send_sem, recv_sem):
+    me, count, peer = peers()
+    leaves, here = dens.shape[0], node_skel.shape[0]
+    greet(count, peer)
+    copies, send = sender(send_sem, recv_sem)
+    for own, wide in ((dens, dens_wide), (skel, skel_wide)):
+        send(own.at[pl.ds(leaves - REACH, REACH)], wide.at[pl.ds(0, REACH)], peer(1)[1])
+        send(own.at[pl.ds(0, REACH)], wide.at[pl.ds(REACH + leaves, REACH)], peer(count - 1)[1])
+    for k in range(1, count):
+        send(node_skel, all_skel.at[pl.ds(me * here, here)], peer(k)[1])
+    dens_wide[REACH : REACH + leaves] = dens[...]
+    dens_wide[leaves + 2 * REACH] = jnp.zeros(dens.shape[1:], dens.dtype)
+    skel_wide[REACH : REACH + leaves] = skel[...]
+    for k in range(here):
+        all_skel[me * here + k] = node_skel[k]
+    for copy in copies:
+        copy.wait()
+
+
+def remote(kernel, name, number, copies, outs, *operands):
+    vmem = pl.BlockSpec(memory_space=pltpu.VMEM)
+    return pl.pallas_call(
+        kernel,
+        out_shape=[jax.ShapeDtypeStruct(*o) for o in outs],
+        in_specs=[vmem] * len(operands),
+        out_specs=[vmem] * len(outs),
+        scratch_shapes=[pltpu.SemaphoreType.DMA((copies,)), pltpu.SemaphoreType.DMA((copies,))],
+        compiler_params=pltpu.CompilerParams(collective_id=number, has_side_effects=True),
+        name=name,
+    )(*operands)
+
+
 def on_device(
     density,
     leaf_target,
@@ -307,23 +383,34 @@
     first_leaf = lax.axis_index(("row", "col")) * leaves
     destination = leaf_target // leaves
     tree_slot = leaf_target % leaves
-    send_order = jnp.argsort(destination, stable=True)
-    outgoing = density[send_order]
-    out_slot = tree_slot[send_order]
-    arrived, arrived_slot = (
-        lax.all_to_all(outgoing, ("row", "col"), split_axis=0, concat_axis=0, tiled=True),
-        lax.all_to_all(out_slot, ("row", "col"), split_axis=0, concat_axis=0, tiled=True),
-    )
-    ordered = arrived[jnp.argsort(arrived_slot)]
-    geo_wide = extended(
-        jnp.pad(geometry, ((0, 2), (0, 0))), ((("row", "col"), 1),), REACH * leaf_size
-    )
+    count = lax.axis_size("row") * lax.axis_size("col")
+    per = leaves // count
+    ids = jnp.arange(leaves, dtype=jnp.int32)
+    earlier = (destination[:, None] == destination) & (ids[:, None] > ids)
+    rank = destination * per + jnp.sum(earlier.astype(jnp.int32), axis=1)
+    placed = rank == ids[:, None]
+    outgoing = density[jnp.sum(jnp.where(placed, ids, 0), axis=1)]
+    out_slot = jnp.sum(jnp.where(placed, tree_slot, 0), axis=1).reshape(count, 1, per)
+    bf16, f32 = jnp.bfloat16, jnp.float32
+    arrived, arrived_slot, geo_wide = remote(
+        exchange_kernel,
+        "exchange",
+        0,
+        2 * count,
+        (
+            (density.shape, bf16),
+            ((count, 1, leaf_size), jnp.int32),
+            ((8, wide * leaf_size), f32),
+        ),
+        outgoing,
+        jnp.pad(out_slot, ((0, 0), (0, 0), (0, leaf_size - per))),
+        jnp.pad(geometry, ((0, 2), (0, 0))),
+    )
+    landed = arrived_slot[:, 0, :per].reshape(leaves)
+    ordered = arrived[jnp.sum(jnp.where(landed == ids[:, None], ids, 0), axis=1)]
     skeleton = jnp.einsum(
         "tnl,trl->tnr", ordered, basis_in, preferred_element_type=jnp.float32
     ).astype(jnp.bfloat16)
-    dens_wide = extended(ordered, ((("row", "col"), 0),), REACH)
-    dens_wide = jnp.pad(dens_wide, ((0, 1), (0, 0), (0, 0)))
-    skel_wide = extended(skeleton, ((("row", "col"), 0),), REACH)
     stacked = (
         skeleton.reshape(nodes_here, children, nrhs_here, rank_size)
         .transpose(0, 2, 1, 3)
@@ -332,9 +419,20 @@
     node_skel = jnp.einsum(
         "pnk,prk->pnr", stacked, transfer, preferred_element_type=jnp.float32
     ).astype(jnp.bfloat16)
-    all_skel = lax.all_gather(
-        node_skel.reshape(nodes_here, nrhs_here * rank_size), ("row", "col"), axis=0, tiled=True
-    ).reshape(-1, nrhs_here, rank_size)
+    dens_wide, skel_wide, all_skel = remote(
+        share_kernel,
+        "share",
+        1,
+        count + 3,
+        (
+            ((wide + 1, nrhs_here, leaf_size), bf16),
+            ((wide, nrhs_here, rank_size), bf16),
+            ((nodes_here * count, nrhs_here, rank_size), bf16),
+        ),
+        ordered,
+        skeleton,
+        node_skel,
+    )
     near = fill(compacted(near_list, REACH - first_leaf, wide))
     far = fill(compacted(far_list, REACH - first_leaf, wide))
     node = fill(compacted(node_list, wide + 1, wide))

time: 129 us -> 108 us (0.84)
  Pallas kernels: 54.3 us -> 90.5 us
  starting transfers between devices: 28.5 us -> 0 us
  blocking collectives: 21.5 us -> 0 us
  waiting for transfers between devices: 6.38 us -> 0 us
  other arithmetic: 9.07 us -> 3.77 us
  local copies, waits for them, and re-layouts: 6.52 us -> 11.4 us
    pallas_call x0 -> x2, Pallas kernels: none -> 35 us  [remote(): pl.pallas_call(kernel, out_shape=[jax.ShapeDtypeStruct(*o) for o in outs]...]
    all_gather x1 -> x0, blocking collectives: 21.5 us -> none  [on_device(): lax.all_gather(node_skel.reshape(nodes_here, nrhs_here * rank_size), ('ro...]
    ppermute x6 -> x0, starting transfers between devices: 15 us -> none  [the longest x3 8.75 us: extended(): lax.ppermute(tail, axis, [(i, (i + 1) % count) for i in range(ends)])]
    all_to_all x2 -> x0, starting transfers between devices: 13.5 us -> none  [the longest x1 7.34 us: on_device(): lax.all_to_all(out_slot, ('row', 'col'), split_axis=0, concat_axis=0, til...]
    all_to_all x2 -> x0, waiting for transfers between devices: 6.37 us -> none  [the longest x1 6.36 us: on_device(): lax.all_to_all(outgoing, ('row', 'col'), split_axis=0, concat_axis=0, til...]
    unnamed x21 -> x32, local copies, waits for them, and re-layouts: 1.27 us -> 4.64 us
    sort x2 -> x0, other arithmetic: 3.29 us -> none  [the longest x1 1.69 us: on_device(): ordered = arrived[jnp.argsort(arrived_slot)]]
    all_to_all x3 -> x0, local copies, waits for them, and re-layouts: 1.37 us -> none  [on_device(): lax.all_to_all(out_slot, ('row', 'col'), split_axis=0, concat_axis=0, til...]
  transfers between devices with their start and end apart: 8 -> 0, of which waited for: 1 -> 0; matrix products, arithmetic and copies ran while one was open for 8% -> 0% of each run, Pallas kernels for 0% -> 0%
where the time goes in v3:
time: 108 us; the launch traced here: 107 us
  Pallas kernels  90.5 us (84%)
  local copies, waits for them, and re-layouts  11.4 us (11%)
  other arithmetic  3.77 us (3%)
  matrix products  1.18 us (1%)
    pallas_call x1, Pallas kernels, field(): pl.pallas_call(functools.partial(field_kernel, wide, nodes, chunk), out_s...  55.5 us
    pallas_call x2, Pallas kernels, remote(): pl.pallas_call(kernel, out_shape=[jax.ShapeDtypeStruct(*o) for o in outs]...  35 us
    unnamed x32, local copies, waits for them, and re-layouts  4.64 us
    gather x1, local copies, waits for them, and re-layouts, on_device(): outgoing = density[jnp.sum(jnp.where(placed, ids, 0), axis=1)]  2.27 us

profile of v3, /device:TPU:1, one launch (start us, length us, event | category | flops | bytes accessed | tf_op | source)
XLA Modules:
  0.0 107.2 jit_solution(8881820502420078532)
XLA Ops:
  0.0 0.0 copy-start
  0.0 0.0 copy-start.14
  0.0 0.7 copy-done.14
  0.7 0.2 convert_reduce_fusion.2
  0.9 0.1 select_reduce_fusion.7
  1.1 0.0 copy-start.9
  1.1 2.3 %gather_fusion = bf16[32,32,128]{2,1,0:T(8,128)(2,1)} fusion(bf16[32,32,128]{2,1,0:T(8,128)(2,1)} %param.10, s32[1024]{0:T(1024)S(1)} %pad_clamp_fusion.1), kind=kCustom, calls=%fused_computation | custom fusion | bytes 524416 | tf_op jit(solution)/shard_map/gather | solution.py:392
  3.3 0.1 reshape.82
  3.4 0.6 pad.17.slots
  4.0 0.0 copy-done.9
  4.0 0.7 pad.18.geo
  4.7 13.0 %exchange.1 = (bf16[32,32,128]{2,1,0:T(8,128)(2,1)}, s32[16,1,128]{2,1,0:T(1,128)}, f32[8,8192]{1,0:T(8,128)}) custom-call(bf16[32,32,128]{2,1,0:T(8,128)(2,1)} %gather_fusion, s32[16,1,128]{2,1,0:T(1,128)} %pad.17.slots, f32[8,4096]{1,0:T(8,128)} %pad.18.geo), custom_call_target="tpu_custom_call" | custom-call | tf_op jit(solution)/shard_map/exchange/pallas_call | solution.py:355
  17.7 0.7 slice_reduce_fusion
  18.4 0.1 eq.124
  18.5 0.1 select_reduce_fusion.6
  18.6 1.6 %gather_fusion.1 = bf16[32,32,128]{2,1,0:T(8,128)(2,1)S(1)} fusion(bf16[32,32,128]{2,1,0:T(8,128)(2,1)} %get-tuple-element.12, s32[1024]{0:T(1024)S(1)} %pad_clamp_fusion), kind=kCustom, calls=%fused_computation.1 | custom fusion | bytes 524416 | tf_op jit(solution)/shard_map/gather | solution.py:410
  20.2 0.0 copy-done
  20.2 0.0 copy-start.7
  20.2 0.4 convolution_convert_fusion.skel
  20.6 0.3 copy-done.7
  20.9 0.0 copy-start.8
  20.9 0.1 copy.34
  21.0 0.6 copy-done.8
  21.6 0.2 reshape.84
  21.8 0.7 copy-done.1
  22.6 0.8 convolution_convert_fusion.1.node_skel
  23.4 22.1 %share.1 = (bf16[65,32,128]{2,1,0:T(8,128)(2,1)}, bf16[64,32,64]{2,1,0:T(8,128)(2,1)}, bf16[64,32,64]{2,1,0:T(8,128)(2,1)}) custom-call(bf16[32,32,128]{2,1,0:T(8,128)(2,1)} %copy-done.7, bf16[32,32,64]{2,1,0:T(8,128)(2,1)} %copy-done.8, bf16[4,32,64]{2,1,0:T(8,128)(2,1)} %convolution_convert_fusion.1.node_skel), custom_call_target="tpu_custom_call" | custom-call | tf_op jit(solution)/shard_map/share/pallas_call | solution.py:355
  45.5 0.0 copy-start.2
  45.5 0.0 copy-done.13
  45.5 0.1 convert_reduce_fusion.5
  45.6 0.0 copy-done.11
  45.6 0.1 copy.28
  45.7 0.1 convert_reduce_fusion.3
  45.8 0.8 fusion.6
  46.6 0.1 select_reduce_fusion.5
  46.7 0.1 convert_reduce_fusion.far_row
  46.8 0.1 select_reduce_fusion.3
  46.9 0.0 copy-done.12
  47.0 0.2 reduce_window_sum.29
  47.1 0.1 copy.30
  47.2 0.1 copy.29
  47.3 0.1 select_reduce_fusion
  47.3 0.1 copy.31
  47.4 0.2 reduce_window_sum.30
  47.7 0.1 select_reduce_fusion.2
  47.8 0.1 copy.23
  47.9 0.1 convert_reduce_fusion.4
  48.0 0.7 fusion.7
  48.7 0.1 select_reduce_fusion.9
  48.8 0.1 convert_reduce_fusion.1.near_row
  48.9 0.1 select_reduce_fusion.4
  49.1 0.2 reduce_window_sum.28
  49.2 0.1 copy.25
  49.3 0.1 copy.24
  49.4 0.1 select_reduce_fusion.1
  49.4 0.1 copy.26
  49.5 0.0 copy-done.10
  49.5 0.0 copy-done.3
  49.6 0.0 copy-done.2
  49.6 0.0 copy-done.6
  49.6 0.0 copy-start.4
  49.6 1.0 copy-done.4
  50.6 1.0 copy-done.5
  51.7 55.5 %field.1 = bf16[32,32,128]{2,1,0:T(8,128)(2,1)} custom-call(s32[32,16]{1,0:T(8,128)S(1)} %compare_select_fusion.1.near_idx, s32[130]{0:T(256)S(1)} %convert_reduce_fusion.1.near_row, s32[130]{0:T(256)S(1)} %compare_select_fusion.6.near_col, s32[1]{0:T(128)} %bitcast.near_total, s32[36,32]{1,0:T(8,128)S(1)} %select_add_fusion.far_idx, ...), custom_call_target="tpu_custom_call" | custom-call | tf_op jit(solution)/shard_map/field/pallas_call | solution.py:246
  (30 shorter events, 0.1 us)
Async XLA Ops:
  0.0 20.2 %copy-start = (bf16[32,64,128]{2,1,0:T(8,128)(2,1)S(1)}, bf16[32,64,128]{2,1,0:T(8,128)(2,1)}, u32[]{:S(2)}) copy-start(bf16[32,64,128]{2,1,0:T(8,128)(2,1)} %param.16) | copy-start | bytes 1572868
  0.0 0.7 copy-start.14
  1.1 3.0 %copy-start.9 = (f32[6,4096]{1,0:T(8,128)S(1)}, f32[6,4096]{1,0:T(8,128)}, u32[]{:S(2)}) copy-start(f32[6,4096]{1,0:T(8,128)} %param.12) | copy-start | bytes 294916
  20.2 0.7 copy-start.7
  20.9 0.7 copy-start.8
  21.6 0.9 copy-start.1
  22.6 22.9 %copy-start.13 = (s32[4,32]{1,0:T(4,128)S(1)}, s32[4,32]{1,0:T(4,128)}, u32[]{:S(2)}) copy-start(s32[4,32]{1,0:T(4,128)} %param.15) | copy-start | bytes 1540
  22.6 23.0 %copy-start.11 = (s32[32,16]{0,1:T(8,128)S(1)}, s32[32,16]{0,1:T(8,128)}, u32[]{:S(2)}) copy-start(s32[32,16]{0,1:T(8,128)} %param.14) | copy-start | bytes 6148
  23.4 23.5 %copy-start.12 = (s32[32,16]{0,1:T(8,128)S(1)}, s32[32,16]{0,1:T(8,128)}, u32[]{:S(2)}) copy-start(s32[32,16]{0,1:T(8,128)} %param.13) | copy-start | bytes 6148
  23.4 26.1 %copy-start.10 = (f32[3,4096]{1,0:T(4,128)S(1)}, f32[3,4096]{1,0:T(4,128)}, u32[]{:S(2)}) copy-start(f32[3,4096]{1,0:T(4,128)} %param.19) | copy-start | bytes 147460
  23.4 26.1 %copy-start.3 = (bf16[32,64,128]{2,1,0:T(8,128)(2,1)S(1)}, bf16[32,64,128]{2,1,0:T(8,128)(2,1)}, u32[]{:S(2)}) copy-start(bf16[32,64,128]{2,1,0:T(8,128)(2,1)} %basis_out.1) | copy-start | bytes 1572868
  45.5 4.1 %copy-start.2 = (bf16[65,32,128]{2,1,0:T(8,128)(2,1)S(1)}, bf16[65,32,128]{2,1,0:T(8,128)(2,1)}, u32[]{:S(2)}) copy-start(bf16[65,32,128]{2,1,0:T(8,128)(2,1)} %get-tuple-element.14.dens) | copy-start | bytes 1597444
  47.6 1.9 %copy-start.6 = (f32[8,8192]{1,0:T(8,128)S(1)}, f32[8,8192]{1,0:T(8,128)}, u32[]{:S(2)}) copy-start(f32[8,8192]{1,0:T(8,128)} %get-tuple-element.11.geo) | copy-start | bytes 786436
  49.6 1.0 copy-start.4
  50.6 1.0 copy-start.5
